TPU v7x, 32 devices: a whole 2x2x4 slice. The times are simulated.
32 devices in a mesh: dp: 2 (over x), dm: 4 (over z), tp: 4 (over y, core).
Axes of the slice: x: 2, y: 2, z: 4, core: 2. Of those that a mesh axis runs over, the one named last changes fastest.
Arguments:
- hidden: bfloat16 [128, 5120], P('dp', 'dm'), parts along dimension 0
- w_q: bfloat16 [5120, 40, 128], P('dm', 'tp')
- w_k: bfloat16 [5120, 40, 128], P('dm', 'tp')
- w_v: bfloat16 [5120, 40, 128], P('dm', 'tp')
- w_o: bfloat16 [40, 128, 5120], P('tp', None, 'dm')
- w_gate: bfloat16 [5120, 13824], P('dm', 'tp')
- w_up: bfloat16 [5120, 13824], P('dm', 'tp')
- w_down: bfloat16 [13824, 5120], P('tp', 'dm')
- norm_attn: bfloat16 [5120], P('dm')
- norm_mlp: bfloat16 [5120], P('dm')
- k_cache: bfloat16 [128, 128, 40, 128], P(('dp', 'dm'), None, 'tp'), parts along dimension 0
- v_cache: bfloat16 [128, 128, 40, 128], P(('dp', 'dm'), None, 'tp'), parts along dimension 0
- seq_lens: int32 [128], P(('dp', 'dm')), parts along dimension 0
- rope_cos: float32 [128, 64], P(('dp', 'dm')), parts along dimension 0
- rope_sin: float32 [128, 64], P(('dp', 'dm')), parts along dimension 0
Outputs:
- output 1: bfloat16 [128, 5120], P('dp', 'dm'), parts along dimension 0
- output 2: bfloat16 [128, 128, 40, 128], P(('dp', 'dm'), None, 'tp'), parts along dimension 0
- output 3: bfloat16 [128, 128, 40, 128], P(('dp', 'dm'), None, 'tp'), parts along dimension 0
There are 2 independent parts. A program takes and returns all parts, laid end to end along the dimension named above; an argument that names none is the same for every part.
All inputs are finite; a program needn't handle non-finite values.
Results may differ from a plain program's by a relative error of at most 0.0106486.
Values are sent between devices in bfloat16 or wider.
A program may use at most 1 GiB of HBM per device.

v0:
```python
import jax
import jax.numpy as jnp
from jax import lax
from jax.sharding import PartitionSpec as P

EPS = 1e-6


def width_norm(x, gain, width_full):
    x_f32 = x.astype(jnp.float32)
    sq_sum = lax.psum(jnp.sum(x_f32 * x_f32, axis=-1, keepdims=True), 'dm')
    scale = lax.rsqrt(sq_sum / width_full + EPS)
    return (x_f32 * scale * gain.astype(jnp.float32)).astype(jnp.bfloat16)


def apply_rope(x, rope_cos, rope_sin):
    half = x.shape[-1] // 2
    first = x[..., :half]
    second = x[..., half:]
    cosine = rope_cos[:, None, :]
    sine = rope_sin[:, None, :]
    return jnp.concatenate([first * cosine - second * sine, second * cosine + first * sine], axis=-1).astype(jnp.bfloat16)


def attend(q_rot, k_rot, v_new, k_cache, v_cache, seq_lens):
    rows, seq_len, kv_local, head_dim = k_cache.shape
    positions = jnp.arange(seq_len)
    write_mask = (positions[None, :] == seq_lens[:, None])[:, :, None, None]
    k_out = jnp.where(write_mask, k_rot[:, None], k_cache)
    v_out = jnp.where(write_mask, v_new[:, None], v_cache)
    q_grp = q_rot.reshape(rows, kv_local, -1, head_dim)
    scores = jnp.einsum('bkgd,bskd->bkgs', q_grp, k_out, preferred_element_type=jnp.float32) * (head_dim ** -0.5)
    key_mask = (positions[None, :] <= seq_lens[:, None])[:, None, None, :]
    scores = jnp.where(key_mask, scores, -1e30)
    attn_probs = jax.nn.softmax(scores, axis=-1).astype(jnp.bfloat16)
    heads = jnp.einsum('bkgs,bskd->bkgd', attn_probs, v_out, preferred_element_type=jnp.float32)
    return heads.astype(jnp.bfloat16).reshape(rows, -1, head_dim), k_out, v_out


def solution(mesh):
    width_shards = mesh.shape['dm']
    row_spec = P('dp', 'dm')
    cache_spec = P(('dp', 'dm'), None, 'tp', None)
    batch_spec = P(('dp', 'dm'))
    rope_spec = P(('dp', 'dm'), None)
    in_specs = (row_spec, P('dm', 'tp', None), P('dm', 'tp', None), P('dm', 'tp', None), P('tp', None, 'dm'), P('dm', 'tp'), P('dm', 'tp'), P('tp', 'dm'), P('dm'), P('dm'), cache_spec, cache_spec, batch_spec, rope_spec, rope_spec)
    out_specs = (row_spec, cache_spec, cache_spec)

    def local_layer(hidden, w_q, w_k, w_v, w_o, w_gate, w_up, w_down, norm_attn, norm_mlp, k_cache, v_cache, seq_lens, rope_cos, rope_sin):
        width_full = hidden.shape[1] * width_shards
        x_norm = width_norm(hidden, norm_attn, width_full)
        q_part = jnp.einsum('bd,dhk->bhk', x_norm, w_q, preferred_element_type=jnp.float32)
        k_part = jnp.einsum('bd,dhk->bhk', x_norm, w_k, preferred_element_type=jnp.float32)
        v_part = jnp.einsum('bd,dhk->bhk', x_norm, w_v, preferred_element_type=jnp.float32)
        q_rows = lax.psum_scatter(q_part, 'dm', scatter_dimension=0, tiled=True)
        k_rows = lax.psum_scatter(k_part, 'dm', scatter_dimension=0, tiled=True)
        v_rows = lax.psum_scatter(v_part, 'dm', scatter_dimension=0, tiled=True)
        q_rot = apply_rope(q_rows, rope_cos, rope_sin)
        k_rot = apply_rope(k_rows, rope_cos, rope_sin)
        attn_heads, k_out, v_out = attend(q_rot, k_rot, v_rows.astype(jnp.bfloat16), k_cache, v_cache, seq_lens)
        heads_all = lax.all_gather(attn_heads, 'dm', axis=0, tiled=True)
        attn_part = jnp.einsum('bhk,hkd->bd', heads_all, w_o, preferred_element_type=jnp.float32)
        attn_out = lax.psum(attn_part, 'tp').astype(jnp.bfloat16)
        h_mid = hidden + attn_out
        x_mlp = width_norm(h_mid, norm_mlp, width_full)
        gate = lax.psum(jnp.dot(x_mlp, w_gate, preferred_element_type=jnp.float32), 'dm')
        up_proj = lax.psum(jnp.dot(x_mlp, w_up, preferred_element_type=jnp.float32), 'dm')
        gated_act = (jax.nn.silu(gate) * up_proj).astype(jnp.bfloat16)
        mlp_out = lax.psum(jnp.dot(gated_act, w_down, preferred_element_type=jnp.float32), 'tp').astype(jnp.bfloat16)
        return h_mid + mlp_out, k_out, v_out

    return jax.shard_map(local_layer, mesh=mesh, in_specs=in_specs, out_specs=out_specs, check_vma=False)
```

profile of v0, /device:TPU:0, one launch (start us, length us, event | category | flops | bytes accessed | tf_op | source)
XLA Modules:
  0.0 261.0 jit_solution(16006440168236904669)
XLA Ops:
  7.2 0.0 copy-start
  7.2 0.0 copy-start.3
  7.2 0.0 reduce-scatter.8.cloned.1.call-start
  7.2 1.2 fusion.9
  8.4 13.5 %psum.42 = f32[64,1]{0,1:T(1,128)S(1)} all-reduce(f32[64,1]{0,1:T(1,128)S(1)} %bitcast.41), channel_id=1, replica_groups=mesh['dp'=2,'dm'=4,'tp'=4] {'dm'}, use_global_device_ids=true, to_apply=%region_1.0 | all-reduce | flops 64 | bytes 512 | tf_op jit(solution)/shard_map/psum | solution.py:11
  22.0 0.7 convert_element_type.47
  22.7 0.0 copy-done
  22.7 0.0 copy-start.7
  22.7 0.0 copy-start.8
  22.7 2.4 fusion.33
  25.1 0.0 copy-start.5
  25.1 0.0 copy-start.6
  25.1 0.0 reduce-scatter.8.cloned.1.call-update
  25.1 0.0 reduce-scatter.6.cloned.1.call-start
  25.1 3.5 %fusion.35 = f32[64,10,128]{2,0,1:T(8,128)} fusion(bf16[1280,10,128]{2,0,1:T(8,128)(2,1)} %param.17, bf16[64,1280]{1,0:T(8,128)(2,1)} %param.15, f32[1280]{0:T(1024)S(1)} %convert_element_type.47, f32[64]{0:T(128)S(1)} %rsqrt_bitcast_fusion.1), kind=kOutput, calls=%fused_computation.53 | convolution fusion | flops 210042880 | bytes 3773696 | tf_op jit(solution)/shard_map/bd,dhk->bhk/dot_general | solution.py:53
  28.6 0.0 reduce-scatter.6.cloned.1.call-update
  28.7 0.0 reduce-scatter.4.cloned.1.call-start
  28.7 0.0 copy-done.3
  28.7 3.4 %fusion.37 = f32[64,10,128]{2,0,1:T(8,128)} fusion(bf16[1280,10,128]{2,0,1:T(8,128)(2,1)} %param.16, bf16[64,1280]{1,0:T(8,128)(2,1)S(1)} %copy-done.3, f32[1280]{0:T(1024)S(1)} %convert_element_type.47, f32[64]{0:T(128)S(1)} %rsqrt_bitcast_fusion.1), kind=kOutput, calls=%fused_computation.54 | convolution fusion | flops 210042880 | bytes 3773696 | tf_op jit(solution)/shard_map/bd,dhk->bhk/dot_general | solution.py:52
  32.1 0.0 reduce-scatter.4.cloned.1.call-update
  32.1 0.0 all-reduce.5.cloned.1.call-start
  32.2 0.0 copy-done.7
  32.2 0.0 copy-done.8
  32.2 0.1 iota_compare_fusion.1
  32.3 11.7 %reduce-scatter.8.cloned.1.call-done = f32[16,10,128]{2,0,1:T(8,128)} async-done(((f32[64,10,128]{2,0,1:T(8,128)}), f32[16,10,128]{2,0,1:T(8,128)}) %reduce-scatter.8.cloned.1.call-update) | async-done | bytes 81936 | tf_op jit(solution)/shard_map/reduce_scatter | solution.py:57
  44.0 0.9 convert_element_type.50
  44.9 20.8 %reduce-scatter.6.cloned.1.call-done = f32[16,10,128]{2,0,1:T(8,128)} async-done(((f32[64,10,128]{2,0,1:T(8,128)}), f32[16,10,128]{2,0,1:T(8,128)}) %reduce-scatter.6.cloned.1.call-update) | async-done | bytes 81936 | tf_op jit(solution)/shard_map/reduce_scatter | solution.py:56
  65.7 21.7 %reduce-scatter.4.cloned.1.call-done = f32[16,10,128]{2,0,1:T(8,128)} async-done(((f32[64,10,128]{2,0,1:T(8,128)}), f32[16,10,128]{2,0,1:T(8,128)}) %reduce-scatter.4.cloned.1.call-update) | async-done | bytes 81936 | tf_op jit(solution)/shard_map/reduce_scatter | solution.py:55
  87.3 0.0 copy-done.5
  87.3 0.0 copy-done.6
  87.3 1.1 subtract_convert_fusion.1
  88.5 0.1 pad_maximum_fusion
  88.6 0.1 maximum_bitcast_fusion
  88.7 6.9 %broadcast_select_fusion.1 = (bf16[16,128,10,128]{3,1,2,0:T(8,128)(2,1)S(1)}, bf16[16,128,10,128]{3,1,2,0:T(8,128)(2,1)}) fusion(bf16[16,128,10,128]{3,1,2,0:T(8,128)(2,1)} %param.25, pred[16,128]{1,0:T(8,128)(4,1)S(1)} %get-tuple-element.16, bf16[16,10,128]{2,1,0:T(8,128)(2,1)S(1)} %copy.20, bf16[16,128,10,128]{3,1,2,0:T(8,128)(2,1)} %param.26, ...), kind=kLoop, calls=%fused_computation.3 | loop fusion | flops 5242880 | bytes 21055488 | tf_op jit(solution)/shard_map/jit(_where)/select_n | solution.py:29
  95.6 0.0 copy-start.2
  95.6 2.4 copy-done.2
  98.0 2.8 %fusion.19 = f32[16,10,1,128]{3,2,1,0:T(1,128)S(1)} fusion(bf16[16,128,10,128]{3,1,2,0:T(8,128)(2,1)S(1)} %get-tuple-element.13, bf16[16,10,128,1]{2,0,1,3:T(8,128)(2,1)S(1)} %maximum_bitcast_fusion), kind=kOutput, calls=%fused_computation.31 | convolution fusion | flops 5242880 | bytes 5365760 | tf_op jit(solution)/shard_map/bkgd,bskd->bkgs/dot_general | solution.py:32
  100.7 0.0 copy-start.4
  100.8 0.2 fusion.6
  101.0 3.9 %fusion.17 = bf16[16,10,1,128]{3,2,1,0:T(2,128)(2,1)S(1)} fusion(bf16[16,128,10,128]{3,1,2,0:T(8,128)(2,1)} %get-tuple-element.14, bf16[16,10,128,1]{2,0,1,3:T(8,128)(2,1)S(1)} %fusion.6), kind=kOutput, calls=%fused_computation.29 | convolution fusion | flops 5242880 | bytes 5324800 | tf_op jit(solution)/shard_map/bkgs,bskd->bkgd/dot_general | solution.py:36
  104.9 13.5 %all_gather.3 = bf16[64,10,128]{2,0,1:T(8,128)(2,1)S(1)} all-gather(bf16[16,10,128]{2,0,1:T(8,128)(2,1)S(1)} %bitcast.39), channel_id=1, replica_groups=mesh['dp'=2,'dm'=4,'tp'=4] {'dm'}, dimensions={0}, use_global_device_ids=true | all-gather | bytes 204800 | tf_op jit(solution)/shard_map/all_gather | solution.py:61
  118.4 2.6 %convolution_bitcast_fusion = f32[64,1280]{1,0:T(8,128)S(1)} fusion(bf16[64,10,128]{2,0,1:T(8,128)(2,1)S(1)} %all_gather.3, bf16[10,128,1280]{2,1,0:T(8,128)(2,1)} %param.19), kind=kOutput, calls=%fused_computation.4 | convolution fusion | flops 209715200 | bytes 3768320 | tf_op jit(solution)/shard_map/bhk,hkd->bd/dot_general | solution.py:62
  121.0 13.5 %all-reduce.6 = bf16[64,1280]{1,0:T(8,128)(2,1)S(1)} all-reduce(f32[64,1280]{1,0:T(8,128)S(1)} %convolution_bitcast_fusion), channel_id=1, replica_groups=mesh['dp'=2,'dm'=4,'tp'=4] {'tp'}, use_global_device_ids=true, to_apply=%region_7.8 | all-reduce | flops 81920 | bytes 491520 | tf_op jit(solution)/shard_map/psum | solution.py:63
  134.5 0.0 copy-done.4
  134.5 0.2 fusion.12
  134.7 8.7 %psum.44 = f32[64,1]{0,1:T(1,128)S(1)} all-reduce(f32[64,1]{0,1:T(1,128)S(1)} %bitcast.40), channel_id=1, replica_groups=mesh['dp'=2,'dm'=4,'tp'=4] {'dm'}, use_global_device_ids=true, to_apply=%region_9.10 | all-reduce | flops 64 | bytes 512 | tf_op jit(solution)/shard_map/psum | solution.py:11
  143.4 6.1 %fusion.23 = f32[64,3456]{1,0:T(8,128)} fusion(bf16[1280,3456]{1,0:T(8,128)(2,1)} %param.21, bf16[64,1280]{1,0:T(8,128)(2,1)S(1)} %get-tuple-element.6, f32[1280]{0:T(1024)S(1)} %convert_element_type.54, f32[64]{0:T(128)S(1)} %rsqrt_bitcast_fusion), kind=kOutput, calls=%fused_computation.38 | convolution fusion | flops 566558720 | bytes 9901312 | tf_op jit(solution)/shard_map/dot_general | solution.py:67
  149.5 6.1 %fusion.25 = f32[64,3456]{1,0:T(8,128)} fusion(bf16[1280,3456]{1,0:T(8,128)(2,1)} %param.20, bf16[64,1280]{1,0:T(8,128)(2,1)S(1)} %get-tuple-element.6, f32[1280]{0:T(1024)S(1)} %convert_element_type.54, f32[64]{0:T(128)S(1)} %rsqrt_bitcast_fusion), kind=kOutput, calls=%fused_computation.39 | convolution fusion | flops 566558720 | bytes 9901312 | tf_op jit(solution)/shard_map/dot_general | solution.py:66
  155.6 0.0 all-reduce.5.cloned.1.call-update
  155.7 75.1 %all-reduce.5.cloned.1.call-done = (f32[64,3456]{1,0:T(8,128)}, f32[64,3456]{1,0:T(8,128)}) async-done(((f32[64,3456]{1,0:T(8,128)}, f32[64,3456]{1,0:T(8,128)}), (f32[64,3456]{1,0:T(8,128)}, f32[64,3456]{1,0:T(8,128)})) %all-reduce.5.cloned.1.call-update) | async-done | bytes 1769488 | tf_op jit(solution)/shard_map/psum | solution.py:67
  230.7 0.0 copy-start.1
  230.7 6.4 %fusion.7 = f32[64,1280]{1,0:T(8,128)} fusion(bf16[3456,1280]{1,0:T(8,128)(2,1)} %param.22, f32[64,3456]{1,0:T(8,128)} %get-tuple-element.3, f32[64,3456]{1,0:T(8,128)} %get-tuple-element.4), kind=kOutput, calls=%fused_computation.11 | convolution fusion | flops 567558144 | bytes 10944512 | tf_op jit(solution)/shard_map/dot_general | solution.py:69
  237.2 15.7 %all-reduce.7 = bf16[64,1280]{1,0:T(8,128)(2,1)} all-reduce(f32[64,1280]{1,0:T(8,128)} %fusion.7), channel_id=1, replica_groups=mesh['dp'=2,'dm'=4,'tp'=4] {'tp'}, use_global_device_ids=true, to_apply=%region_12.13 | all-reduce | flops 81920 | bytes 491520 | tf_op jit(solution)/shard_map/psum | solution.py:69
  252.8 1.6 add.55
  254.5 0.0 copy-done.1
  (6 shorter events, 0.1 us)
Async XLA Ops:
  7.2 15.5 %copy-start = (bf16[1280,10,128]{2,0,1:T(8,128)(2,1)S(1)}, bf16[1280,10,128]{2,0,1:T(8,128)(2,1)}, u32[]{:S(2)}) copy-start(bf16[1280,10,128]{2,0,1:T(8,128)(2,1)} %param.18) | copy-start | bytes 9830404
  7.2 21.5 %copy-start.3 = (bf16[64,1280]{1,0:T(8,128)(2,1)S(1)}, bf16[64,1280]{1,0:T(8,128)(2,1)}, u32[]{:S(2)}) copy-start(bf16[64,1280]{1,0:T(8,128)(2,1)} %param.15) | copy-start | bytes 491524
  7.2 36.8 %reduce-scatter.8.cloned.1.call-start = ((), (), s32[]{:S(2)}) async-start(), calls=%async_computation.5 | async-start | bytes 409600 | tf_op jit(solution)/shard_map/reduce_scatter | solution.py:57
  22.7 9.5 %copy-start.7 = (bf16[1280]{0:T(1024)(128)(2,1)S(1)}, bf16[1280]{0:T(1024)(128)(2,1)}, u32[]{:S(2)}) copy-start(bf16[1280]{0:T(1024)(128)(2,1)} %param.24) | copy-start | bytes 7684
  22.7 9.5 %copy-start.8 = (s32[16]{0:T(128)S(1)}, s32[16]{0:T(128)}, u32[]{:S(2)}) copy-start(s32[16]{0:T(128)} %param.27) | copy-start | bytes 196
  25.1 62.3 %copy-start.5 = (f32[16,64]{1,0:T(8,128)S(1)}, f32[16,64]{1,0:T(8,128)}, u32[]{:S(2)}) copy-start(f32[16,64]{1,0:T(8,128)} %param.29) | copy-start | bytes 12292
  25.1 62.3 %copy-start.6 = (f32[16,64]{1,0:T(8,128)S(1)}, f32[16,64]{1,0:T(8,128)}, u32[]{:S(2)}) copy-start(f32[16,64]{1,0:T(8,128)} %param.28) | copy-start | bytes 12292
  25.1 40.6 %reduce-scatter.6.cloned.1.call-start = ((), (), s32[]{:S(2)}) async-start(), calls=%async_computation.4 | async-start | bytes 409600 | tf_op jit(solution)/shard_map/reduce_scatter | solution.py:56
  28.7 58.7 %reduce-scatter.4.cloned.1.call-start = ((), (), s32[]{:S(2)}) async-start(), calls=%async_computation.3 | async-start | bytes 409600 | tf_op jit(solution)/shard_map/reduce_scatter | solution.py:55
  32.1 198.6 %all-reduce.5.cloned.1.call-start = ((), (), s32[]{:S(2)}) async-start(), calls=%async_computation.6 | async-start | bytes 3538944 | tf_op jit(solution)/shard_map/psum | solution.py:67
  95.6 2.4 copy-start.2
  100.7 33.7 %copy-start.4 = (bf16[64,1280]{1,0:T(8,128)(2,1)S(1)}, bf16[64,1280]{1,0:T(8,128)(2,1)}, u32[]{:S(2)}) copy-start(bf16[64,1280]{1,0:T(8,128)(2,1)} %param.15) | copy-start | bytes 491524
  230.7 23.7 %copy-start.1 = (bf16[1280,10,128]{2,0,1:T(8,128)(2,1)S(1)}, bf16[1280,10,128]{2,0,1:T(8,128)(2,1)}, u32[]{:S(2)}) copy-start(bf16[1280,10,128]{2,0,1:T(8,128)(2,1)} %param.18) | copy-start | bytes 9830404
Sparse Core Ops, SparseCore 0:
  25.2 18.7 reduce-scatter.7
  46.9 18.7 reduce-scatter.5
  68.5 18.7 reduce-scatter.3
  155.8 74.9 all-reduce.4
where the time goes:
time: 262 us; the launch traced here: 261 us
  waiting for transfers between devices  129 us (49%)
  blocking collectives  64.8 us (25%)
  matrix products  37.4 us (14%)
  between operations  13.9 us (5%)
  other arithmetic  13.1 us (5%)
    psum x1, waiting for transfers between devices, local_layer(): lax.psum(jnp.dot(x_mlp, w_up, preferred_element_type=jnp.float32), 'dm')  75.1 us
    psum x2, blocking collectives, width_norm(): sq_sum = lax.psum(jnp.sum(x_f32 * x_f32, axis=-1, keepdims=True), 'dm')  22.2 us
    reduce_scatter x1, waiting for transfers between devices, local_layer(): q_rows = lax.psum_scatter(q_part, 'dm', scatter_dimension=0, tiled=True)  21.7 us
    reduce_scatter x1, waiting for transfers between devices, local_layer(): k_rows = lax.psum_scatter(k_part, 'dm', scatter_dimension=0, tiled=True)  20.8 us
    psum x1, blocking collectives, local_layer(): lax.psum(jnp.dot(gated_act, w_down, preferred_element_type=jnp.float32),...  15.7 us
    psum x1, blocking collectives, local_layer(): attn_out = lax.psum(attn_part, 'tp').astype(jnp.bfloat16)  13.5 us
    all_gather x1, blocking collectives, local_layer(): heads_all = lax.all_gather(attn_heads, 'dm', axis=0, tiled=True)  13.5 us
    reduce_scatter x1, waiting for transfers between devices, local_layer(): v_rows = lax.psum_scatter(v_part, 'dm', scatter_dimension=0, tiled=True)  11.7 us
  transfers between devices with their start and end apart: 4, of which 4 were waited for; matrix products, arithmetic and copies ran while one was open for 3% of the time, Pallas kernels for 0%

commit v1 on v0

v1 whole, which is shorter than its diff:
```python
import functools

import jax
import jax.numpy as jnp
from jax import lax
from jax.experimental import pallas as pl
from jax.experimental.pallas import tpu as pltpu
from jax.sharding import PartitionSpec as P

EPS = 1e-6
MESH = pl.DeviceIdType.MESH
F32 = jnp.float32
BF16 = jnp.bfloat16
NZ = 4
A_LAG = 2
E_LAG = 4
COL = 128
RCOL = 256


def remote(src, dst, send_sem, recv_sem, **where):
    return pltpu.make_async_remote_copy(src_ref=src, dst_ref=dst, send_sem=send_sem, recv_sem=recv_sem, device_id=where, device_id_type=MESH)


def barrier(z, tp):
    sem = pltpu.get_barrier_semaphore()
    count = 0
    for k in range(1, NZ):
        pl.semaphore_signal(sem, inc=1, device_id={'dm': lax.rem(z + k, NZ)}, device_id_type=MESH)
        count += 1
    if tp is not None:
        for k in (1, 2):
            pl.semaphore_signal(sem, inc=1, device_id={'tp': partner(tp, k)}, device_id_type=MESH)
            count += 1
    pl.semaphore_wait(sem, count)


def partner(tp, k):
    if k == 1:
        return tp + 1 - 2 * lax.rem(tp, 2)
    return lax.rem(tp + 2, 4)


def exchange_sq(z, x, sq_buf, send, recv):
    rows = x.shape[0]
    lane = lax.broadcasted_iota(jnp.int32, (rows, 128), 1)
    row = lax.broadcasted_iota(jnp.int32, (rows, 128), 0)
    col = jnp.sum(x * x, axis=-1, keepdims=True)
    packed = jnp.sum(jnp.where(lane == row, col, 0.0), axis=0, keepdims=True)
    sq_buf[z] = jnp.broadcast_to(packed, (8, 128))
    for k in range(1, NZ):
        peer = lax.rem(z + k, NZ)
        remote(sq_buf.at[z], sq_buf.at[z], send.at[peer], recv.at[z], dm=peer).start()
    for k in range(1, NZ):
        peer = lax.rem(z + k, NZ)
        cp = remote(sq_buf.at[peer], sq_buf.at[peer], send.at[peer], recv.at[peer], dm=peer)
        cp.wait_recv()
        cp.wait_send()
    total = (sq_buf[0] + sq_buf[1]) + (sq_buf[2] + sq_buf[3])
    wide = jnp.broadcast_to(total[0:1], (rows, 128))
    return jnp.sum(jnp.where(lane == row, wide, 0.0), axis=1, keepdims=True)


def qkv_kernel(hid, gain, wq, wk, wv, cos, sin, out, wbuf, part, rbuf, lbuf, x_buf, sq_buf, w_sem, sq_s, sq_r, rs, rr, ls, lr):
    z = lax.axis_index('dm')
    heads = wq.shape[0]
    width = hid.shape[1] * NZ
    for h in range(heads):
        for i, w in enumerate((wq, wk, wv)):
            pltpu.make_async_copy(w.at[h], wbuf.at[i, h], w_sem.at[i, h]).start()
    barrier(z, None)
    x = hid[...].astype(F32)
    sq = exchange_sq(z, x, sq_buf, sq_s, sq_r)
    x_buf[...] = (x * lax.rsqrt(sq / width + EPS) * gain[...].astype(F32)).astype(BF16)
    cos2 = jnp.concatenate([cos[...], cos[...]], axis=-1)
    sin2 = jnp.concatenate([-sin[...], sin[...]], axis=-1)

    def right(d, p):
        return remote(part.at[d, p], rbuf.at[d, p], rs.at[d, p], rr.at[d, p], dm=lax.rem(z + 1, NZ))

    def left(d, p):
        return remote(part.at[d, p], lbuf.at[d, p], ls.at[d, p], lr.at[d, p], dm=lax.rem(z + NZ - 1, NZ))

    def slot(t, carry):
        @pl.when(t < heads)
        def _():
            for i, w in enumerate((wq, wk, wv)):
                pltpu.make_async_copy(w.at[t], wbuf.at[i, t], w_sem.at[i, t]).wait()
                y = jnp.dot(x_buf[...], wbuf[i, t], preferred_element_type=F32)
                for d in range(NZ):
                    part[d, t, :, i * 128:(i + 1) * 128] = y[d * 16:(d + 1) * 16]

        p = t - A_LAG * z

        @pl.when((p >= 0) & (p < heads))
        def _():
            for d in (3, 2, 1):
                @pl.when((z > 0) & (z <= d))
                def _(d=d):
                    right(d, p).wait_recv()
                    part[d, p] = part[d, p] + rbuf[d, p]

                @pl.when(z < d)
                def _(d=d):
                    right(d, p).start()

        b = t - A_LAG * (NZ - 1 - z)

        @pl.when((b >= 0) & (b < heads))
        def _():
            for d in (0, 1, 2):
                @pl.when((z < NZ - 1) & (z >= d))
                def _(d=d):
                    left(d, b).wait_recv()
                    part[d, b] = part[d, b] + lbuf[d, b]

                @pl.when(z > d)
                def _(d=d):
                    left(d, b).start()

        f = t - A_LAG * jnp.maximum(z, NZ - 1 - z)

        @pl.when((f >= 0) & (f < heads))
        def _():
            q = part[z, f, :, 0:128]
            k = part[z, f, :, 128:256]
            out[0, f] = (q * cos2 + pltpu.roll(q, 64, 1) * sin2).astype(BF16)
            out[1, f] = (k * cos2 + pltpu.roll(k, 64, 1) * sin2).astype(BF16)
            out[2, f] = part[z, f, :, 256:384].astype(BF16)

        return carry

    lax.fori_loop(0, heads + A_LAG * (NZ - 1), slot, 0)

    def drain(p, carry):
        for d in range(NZ):
            @pl.when(z < d)
            def _(d=d):
                right(d, p).wait_send()

            @pl.when(z > d)
            def _(d=d):
                left(d, p).wait_send()

        return carry

    lax.fori_loop(0, heads, drain, 0)


def qkv_call(hid, gain, wq, wk, wv, cos, sin):
    heads, width, hd = wq.shape
    rows = hid.shape[0]
    vm = pl.BlockSpec(memory_space=pltpu.VMEM)
    hbm = pl.BlockSpec(memory_space=pltpu.HBM)
    dma = pltpu.SemaphoreType.DMA
    return pl.pallas_call(
        qkv_kernel,
        name='qkv_rs',
        out_shape=jax.ShapeDtypeStruct((3, heads, rows // NZ, hd), BF16),
        in_specs=[vm, vm, hbm, hbm, hbm, vm, vm],
        out_specs=vm,
        scratch_shapes=[
            pltpu.VMEM((3, heads, width, hd), BF16),
            pltpu.VMEM((NZ, heads, rows // NZ, 3 * hd), F32),
            pltpu.VMEM((NZ, heads, rows // NZ, 3 * hd), F32),
            pltpu.VMEM((NZ, heads, rows // NZ, 3 * hd), F32),
            pltpu.VMEM((rows, width), BF16),
            pltpu.VMEM((NZ, 8, 128), F32),
            dma((3, heads)),
            dma((NZ,)), dma((NZ,)),
            dma((NZ, heads)), dma((NZ, heads)), dma((NZ, heads)), dma((NZ, heads)),
        ],
        compiler_params=pltpu.CompilerParams(collective_id=0, has_side_effects=True, vmem_limit_bytes=20 * 2**20),
        cost_estimate=pl.CostEstimate(flops=2 * rows * width * heads * 3 * hd, bytes_accessed=80_000_000, transcendentals=0),
    )(hid, gain, wq, wk, wv, cos, sin)


def attn_kernel(lens, qkv, k_in, v_in, o, k_out, v_out):
    rows, heads, slots, hd = k_in.shape
    row = lax.broadcasted_iota(jnp.int32, (rows, slots), 0)
    pos = lax.broadcasted_iota(jnp.int32, (rows, slots), 1)
    tile_pos = lax.broadcasted_iota(jnp.int32, (16, hd), 0)
    length = jnp.zeros((rows, slots), jnp.int32)
    for r in range(rows):
        length = jnp.where(row == r, lens[r], length)
    at_len = pos == length
    seen = pos <= length

    def head(h, carry):
        q = qkv[0, h]
        k_new = qkv[1, h].astype(F32)
        v_new = qkv[2, h].astype(F32)
        s = jnp.zeros((rows, slots), F32)
        for r in range(rows):
            y = lax.dot_general(q, k_in[r, h], (((1,), (1,)), ((), ())), preferred_element_type=F32)
            s = jnp.where(row == r, y, s)
        s_new = jnp.sum(q.astype(F32) * k_new, axis=-1, keepdims=True)
        s = jnp.where(at_len, s_new, s) * (hd ** -0.5)
        s = jnp.where(seen, s, -1e30)
        e = jnp.exp(s - jnp.max(s, axis=-1, keepdims=True))
        prob = (e / jnp.sum(e, axis=-1, keepdims=True)).astype(BF16)
        prob32 = prob.astype(F32)
        p_new = jnp.sum(jnp.where(at_len, prob32, 0.0), axis=-1, keepdims=True)
        p_old = jnp.where(at_len, 0.0, prob32).astype(BF16)
        acc = jnp.zeros((rows, hd), F32)
        for r in range(rows):
            y = jnp.dot(p_old, v_in[r, h], preferred_element_type=F32)
            acc = jnp.where(row == r, y, acc)
        o[h] = (acc + p_new * v_new).astype(BF16)
        for r in range(rows):
            k_out[r, h] = k_in[r, h]
            v_out[r, h] = v_in[r, h]
            base = pl.multiple_of((lens[r] // 16) * 16, 16)
            hit = tile_pos == lens[r] - base
            old = k_in[r, h, pl.ds(base, 16), :].astype(F32)
            k_out[r, h, pl.ds(base, 16), :] = jnp.where(hit, k_new[r:r + 1], old).astype(BF16)
            old = v_in[r, h, pl.ds(base, 16), :].astype(F32)
            v_out[r, h, pl.ds(base, 16), :] = jnp.where(hit, v_new[r:r + 1], old).astype(BF16)
        return carry

    lax.fori_loop(0, heads, head, 0)


def attn_call(lens, qkv, k_cache, v_cache):
    rows, heads, slots, hd = k_cache.shape
    vm = pl.BlockSpec(memory_space=pltpu.VMEM)
    cache = jax.ShapeDtypeStruct(k_cache.shape, BF16)
    return pl.pallas_call(
        attn_kernel,
        name='attn',
        out_shape=[jax.ShapeDtypeStruct((heads, rows, hd), BF16), cache, cache],
        in_specs=[pl.BlockSpec(memory_space=pltpu.SMEM), vm, vm, vm],
        out_specs=[vm, vm, vm],
        compiler_params=pltpu.CompilerParams(vmem_limit_bytes=28 * 2**20),
        cost_estimate=pl.CostEstimate(flops=4 * rows * heads * slots * hd, bytes_accessed=8 * rows * heads * slots * hd, transcendentals=rows * heads * slots),
    )(lens, qkv, k_cache, v_cache)


def mlp_kernel(o_mine, hid, gain, wo, wg, wu, wd, out,
               wo_b, wg_b, wu_b, wd_b, o_all, part, r1, s_buf, r2, h_mid, x_buf, pbuf, rbuf, lbuf, mbuf, sq_buf,
               w_sem, g_sem, o_s, o_r, a_s, a_r, b_s, b_r, c_s, c_r, sq_s, sq_r,
               rs, rr, ls, lr, mr_s, mr_r, ml_s, ml_r):
    z = lax.axis_index('dm')
    tp = lax.axis_index('tp')
    rows, width = hid.shape
    half = rows // 2
    per = rows // NZ
    heads, hd = o_mine.shape[0], o_mine.shape[2]
    ff = wg.shape[1]
    n_col = ff // COL
    n_grp = g_sem.shape[1]
    grp = ff // n_grp
    n_red = width // RCOL
    core = lax.rem(tp, 2)
    sib, across = partner(tp, 1), partner(tp, 2)
    mine = pl.ds(pl.multiple_of(core * half, half), half)
    other = pl.ds(pl.multiple_of((1 - core) * half, half), half)

    load_o = pltpu.make_async_copy(wo, wo_b, w_sem.at[0])
    load_d = pltpu.make_async_copy(wd, wd_b, w_sem.at[1])

    def load(i, g):
        src, dst = ((wg, wg_b), (wu, wu_b))[i]
        cols = pl.ds(pl.multiple_of(g * grp, COL), grp)
        return pltpu.make_async_copy(src.at[:, cols], dst.at[:, cols], g_sem.at[i, g])

    load_o.start()
    for g in range(n_grp):
        load(0, g).start()
        load(1, g).start()
    load_d.start()
    barrier(z, tp)

    def o_copy(frm, to):
        return remote(o_mine, o_all.at[frm], o_s.at[to], o_r.at[frm], dm=to)

    for k in (2, 1, 3):
        o_copy(z, lax.rem(z + k, NZ)).start()
    o_all[z] = o_mine[...]
    for k in (1, 3, 2):
        o_copy(lax.rem(z + k, NZ), lax.rem(z + k, NZ)).wait_recv()

    def reduce_tp(step, lhs, w_ref, base, dst, add):
        def a_copy(j):
            return remote(part.at[j, other], r1.at[step, j], a_s.at[step, j], a_r.at[step, j], tp=sib)

        def b_copy(j):
            return remote(s_buf.at[step, j], r2.at[step, j], b_s.at[step, j], b_r.at[step, j], tp=across)

        def c_copy(j):
            view = dst.at[mine, pl.ds(j * RCOL, RCOL)]
            return remote(view, view, c_s.at[step, j], c_r.at[step, j], tp=sib)

        def c_arrival(j):
            view = dst.at[other, pl.ds(j * RCOL, RCOL)]
            return remote(view, view, c_s.at[step, j], c_r.at[step, j], tp=sib)

        for j in range(n_red):
            part[j] = jnp.dot(lhs, w_ref[:, j * RCOL:(j + 1) * RCOL], preferred_element_type=F32)
            a_copy(j).start()
        for j in range(n_red):
            a_copy(j).wait_recv()
            s_buf[step, j] = part[j, mine] + r1[step, j]
            b_copy(j).start()
        for j in range(n_red):
            b_copy(j).wait_recv()
            total = (s_buf[step, j] + r2[step, j]).astype(BF16)
            cols = pl.ds(j * RCOL, RCOL)
            dst[mine, cols] = (base[mine, cols].astype(F32) + total.astype(F32)).astype(BF16)
            c_copy(j).start()
        for j in range(n_red):
            c_arrival(j).wait_recv()
            a_copy(j).wait_send()
            b_copy(j).wait_send()
            c_copy(j).wait_send()

    load_o.wait()
    o_cat = jnp.concatenate([jnp.concatenate([o_all[d, h] for h in range(heads)], axis=1) for d in range(NZ)], axis=0)
    x_buf[...] = o_cat
    reduce_tp(0, x_buf[...], wo_b, hid, h_mid, None)
    for k in range(1, NZ):
        o_copy(z, lax.rem(z + k, NZ)).wait_send()

    x = h_mid[...].astype(F32)
    sq = exchange_sq(z, x, sq_buf, sq_s, sq_r)
    x_buf[...] = (x * lax.rsqrt(sq / (width * NZ) + EPS) * gain[...].astype(F32)).astype(BF16)

    low, high = pl.ds(0, half), pl.ds(half, half)
    nxt, prv = lax.rem(z + 1, NZ), lax.rem(z + NZ - 1, NZ)

    def right(c):
        return remote(pbuf.at[c, 1], rbuf.at[c], rs.at[c], rr.at[c], dm=nxt)

    def left(c):
        return remote(pbuf.at[c, 0], lbuf.at[c], ls.at[c], lr.at[c], dm=prv)

    def cols_of(c):
        return pl.ds(pl.multiple_of(c * COL, COL), COL)

    def m_left(c):
        view = mbuf.at[high, cols_of(c)]
        return remote(view, view, mr_s.at[c], mr_r.at[c], dm=prv)

    def m_right(c):
        view = mbuf.at[low, cols_of(c)]
        return remote(view, view, ml_s.at[c], ml_r.at[c], dm=nxt)

    def gated(a):
        g, u = a[:, :COL], a[:, COL:]
        return (g * (1.0 / (1.0 + jnp.exp(-g))) * u).astype(BF16)

    def slot(t, carry):
        @pl.when(t < n_col)
        def _():
            per_grp = n_col // n_grp

            @pl.when(lax.rem(t, per_grp) == 0)
            def _():
                load(0, t // per_grp).wait()
                load(1, t // per_grp).wait()

            g = jnp.dot(x_buf[...], wg_b[:, cols_of(t)], preferred_element_type=F32)
            u = jnp.dot(x_buf[...], wu_b[:, cols_of(t)], preferred_element_type=F32)
            pbuf[t, 0, :, 0:COL] = g[:half]
            pbuf[t, 1, :, 0:COL] = g[half:]
            pbuf[t, 0, :, COL:] = u[:half]
            pbuf[t, 1, :, COL:] = u[half:]

        c = t - E_LAG * z

        @pl.when((c >= 0) & (c < n_col))
        def _():
            @pl.when(z > 0)
            def _():
                right(c).wait_recv()
                pbuf[c, 1] = pbuf[c, 1] + rbuf[c]

            @pl.when(z < NZ - 1)
            def _():
                right(c).start()

            @pl.when(z == NZ - 1)
            def _():
                mbuf[high, cols_of(c)] = gated(pbuf[c, 1])
                m_left(c).start()

        b = t - E_LAG * (NZ - 1 - z)

        @pl.when((b >= 0) & (b < n_col))
        def _():
            @pl.when(z < NZ - 1)
            def _():
                left(b).wait_recv()
                pbuf[b, 0] = pbuf[b, 0] + lbuf[b]

            @pl.when(z > 0)
            def _():
                left(b).start()

            @pl.when(z == 0)
            def _():
                mbuf[low, cols_of(b)] = gated(pbuf[b, 0])
                m_right(b).start()

        e = t - E_LAG * (2 * NZ - 2 - z)

        @pl.when((e >= 0) & (e < n_col) & (z < NZ - 1))
        def _():
            m_left(e).wait_recv()

            @pl.when(z > 0)
            def _():
                m_left(e).start()

        f = t - E_LAG * (NZ - 1 + z)

        @pl.when((f >= 0) & (f < n_col) & (z > 0))
        def _():
            m_right(f).wait_recv()

            @pl.when(z < NZ - 1)
            def _():
                m_right(f).start()

        return carry

    lax.fori_loop(0, n_col + E_LAG * (2 * NZ - 2), slot, 0)
    load_d.wait()
    reduce_tp(1, mbuf[...], wd_b, h_mid, out, None)

    def drain(c, carry):
        @pl.when(z < NZ - 1)
        def _():
            right(c).wait_send()
            m_right(c).wait_send()

        @pl.when(z > 0)
        def _():
            left(c).wait_send()
            m_left(c).wait_send()

        return carry

    lax.fori_loop(0, n_col, drain, 0)


def mlp_call(o_mine, hid, gain, wo, wg, wu, wd):
    rows, width = hid.shape
    heads, per, hd = o_mine.shape
    ff = wg.shape[1]
    n_col, n_red = ff // COL, width // RCOL
    n_grp = 9 if n_col % 9 == 0 else 1
    half = rows // 2
    vm = pl.BlockSpec(memory_space=pltpu.VMEM)
    hbm = pl.BlockSpec(memory_space=pltpu.HBM)
    dma = pltpu.SemaphoreType.DMA
    return pl.pallas_call(
        mlp_kernel,
        name='mlp',
        out_shape=jax.ShapeDtypeStruct((rows, width), BF16),
        in_specs=[vm, vm, vm, hbm, hbm, hbm, hbm],
        out_specs=vm,
        scratch_shapes=[
            pltpu.VMEM(wo.shape, BF16), pltpu.VMEM(wg.shape, BF16), pltpu.VMEM(wu.shape, BF16), pltpu.VMEM(wd.shape, BF16),
            pltpu.VMEM((NZ, heads, per, hd), BF16),
            pltpu.VMEM((n_red, rows, RCOL), F32),
            pltpu.VMEM((2, n_red, half, RCOL), F32),
            pltpu.VMEM((2, n_red, half, RCOL), F32),
            pltpu.VMEM((2, n_red, half, RCOL), F32),
            pltpu.VMEM((rows, width), BF16),
            pltpu.VMEM((rows, width), BF16),
            pltpu.VMEM((n_col, 2, half, 2 * COL), F32),
            pltpu.VMEM((n_col, half, 2 * COL), F32),
            pltpu.VMEM((n_col, half, 2 * COL), F32),
            pltpu.VMEM((rows, ff), BF16),
            pltpu.VMEM((NZ, 8, 128), F32),
            dma((2,)), dma((2, n_grp)),
            dma((NZ,)), dma((NZ,)),
            dma((2, n_red)), dma((2, n_red)), dma((2, n_red)), dma((2, n_red)), dma((2, n_red)), dma((2, n_red)),
            dma((NZ,)), dma((NZ,)),
            dma((n_col,)), dma((n_col,)), dma((n_col,)), dma((n_col,)),
            dma((n_col,)), dma((n_col,)), dma((n_col,)), dma((n_col,)),
        ],
        compiler_params=pltpu.CompilerParams(collective_id=1, has_side_effects=True, vmem_limit_bytes=44 * 2**20),
        cost_estimate=pl.CostEstimate(flops=2 * rows * width * (width + 3 * ff), bytes_accessed=150_000_000, transcendentals=0),
    )(o_mine, hid, gain, wo, wg, wu, wd)


def solution(mesh):
    row_spec = P('dp', 'dm')
    cache_spec = P(('dp', 'dm'), None, 'tp', None)
    batch_spec = P(('dp', 'dm'))
    rope_spec = P(('dp', 'dm'), None)
    in_specs = (row_spec, P('dm', 'tp', None), P('dm', 'tp', None), P('dm', 'tp', None), P('tp', None, 'dm'), P('dm', 'tp'), P('dm', 'tp'), P('tp', 'dm'), P('dm'), P('dm'), cache_spec, cache_spec, batch_spec, rope_spec, rope_spec)
    out_specs = (row_spec, cache_spec, cache_spec)

    def local_layer(hidden, w_q, w_k, w_v, w_o, w_gate, w_up, w_down, norm_attn, norm_mlp, k_cache, v_cache, seq_lens, rope_cos, rope_sin):
        by_head = [w.transpose(1, 0, 2) for w in (w_q, w_k, w_v)]
        qkv = qkv_call(hidden, norm_attn.reshape(1, -1), *by_head, rope_cos, rope_sin)
        heads, k_out, v_out = attn_call(seq_lens, qkv, k_cache.transpose(0, 2, 1, 3), v_cache.transpose(0, 2, 1, 3))
        h_out = mlp_call(heads, hidden, norm_mlp.reshape(1, -1), w_o.reshape(-1, w_o.shape[-1]), w_gate, w_up, w_down)
        return h_out, k_out.transpose(0, 2, 1, 3), v_out.transpose(0, 2, 1, 3)

    return jax.shard_map(local_layer, mesh=mesh, in_specs=in_specs, out_specs=out_specs, check_vma=False)
```

time: 262 us -> 132 us (0.50)
  waiting for transfers between devices: 129 us -> 0 us
  Pallas kernels: 0 us -> 118 us
  blocking collectives: 64.8 us -> 0 us
  matrix products: 37.4 us -> 0 us
  between operations: 13.9 us -> 0.7 us
  other arithmetic: 13.1 us -> 0.01 us
  local copies, waits for them, and re-layouts: 2.44 us -> 13 us
    pallas_call x0 -> x3, Pallas kernels: none -> 118 us  [the longest x1 68.2 us: mlp_call(): pl.pallas_call(mlp_kernel, name='mlp', out_shape=jax.ShapeDtypeStruct((ro...]
    psum x1 -> x0, waiting for transfers between devices: 75.1 us -> none  [local_layer(): lax.psum(jnp.dot(x_mlp, w_up, preferred_element_type=jnp.float32), 'dm')]
    reduce_scatter x3 -> x0, waiting for transfers between devices: 54.1 us -> none  [the longest x1 21.7 us: local_layer(): q_rows = lax.psum_scatter(q_part, 'dm', scatter_dimension=0, tiled=True)]
    psum x4 -> x0, blocking collectives: 51.3 us -> none  [the longest x2 22.2 us: width_norm(): sq_sum = lax.psum(jnp.sum(x_f32 * x_f32, axis=-1, keepdims=True), 'dm')]
    dot_general x9 -> x0, matrix products: 37.4 us -> none  [the longest x1 6.43 us: local_layer(): jnp.dot(gated_act, w_down, preferred_element_type=jnp.float32)]
    all_gather x1 -> x0, blocking collectives: 13.5 us -> none  [local_layer(): heads_all = lax.all_gather(attn_heads, 'dm', axis=0, tiled=True)]
    unnamed x18 -> x25, local copies, waits for them, and re-layouts: 2.4 us -> 11.3 us
    select_n x1 -> x0, other arithmetic: 6.92 us -> none  [attend(): k_out = jnp.where(write_mask, k_rot[:, None], k_cache)]
  transfers between devices with their start and end apart: 4 -> 0, of which waited for: 4 -> 0; matrix products, arithmetic and copies ran while one was open for 3% -> 0% of each run, Pallas kernels for 0% -> 0%
where the time goes in v1:
time: 132 us
  Pallas kernels  118 us (89%)
  local copies, waits for them, and re-layouts  13 us (10%)
    pallas_call x1, Pallas kernels, mlp_call(): pl.pallas_call(mlp_kernel, name='mlp', out_shape=jax.ShapeDtypeStruct((ro...  68.2 us
    pallas_call x1, Pallas kernels, qkv_call(): pl.pallas_call(qkv_kernel, name='qkv_rs', out_shape=jax.ShapeDtypeStruct(...  37 us
    pallas_call x1, Pallas kernels, attn_call(): pl.pallas_call(attn_kernel, name='attn', out_shape=[jax.ShapeDtypeStruct(...  12.9 us
    unnamed x25, local copies, waits for them, and re-layouts  11.3 us

profile of v1, /device:TPU:0, one launch (start us, length us, event | category | flops | bytes accessed | tf_op | source)
XLA Modules:
  0.0 131.7 jit_solution(11781630670913027383)
XLA Ops:
  0.6 0.0 slice-start
  0.6 0.8 reshape.15.gain
  1.5 0.9 reshape.16.gain
  2.4 0.0 copy-start.2
  2.4 1.9 %copy-done.2 = bf16[1280,10,128]{2,0,1:T(8,128)(2,1)S(1)} copy-done((bf16[1280,10,128]{2,0,1:T(8,128)(2,1)S(1)}, bf16[1280,10,128]{2,0,1:T(8,128)(2,1)}, u32[]{:S(2)}) %copy-start.2) | copy-done | bytes 3276824
  4.3 0.0 copy-start.3
  4.3 1.9 %copy-done.3 = bf16[1280,10,128]{2,0,1:T(8,128)(2,1)S(1)} copy-done((bf16[1280,10,128]{2,0,1:T(8,128)(2,1)S(1)}, bf16[1280,10,128]{2,0,1:T(8,128)(2,1)}, u32[]{:S(2)}) %copy-start.3) | copy-done | bytes 3276824
  6.2 0.0 copy-start.4
  6.2 1.9 %copy-done.4 = bf16[1280,10,128]{2,0,1:T(8,128)(2,1)S(1)} copy-done((bf16[1280,10,128]{2,0,1:T(8,128)(2,1)S(1)}, bf16[1280,10,128]{2,0,1:T(8,128)(2,1)}, u32[]{:S(2)}) %copy-start.4) | copy-done | bytes 3276824
  8.1 0.0 copy-start.5
  8.2 0.9 copy-done.5
  9.1 0.0 copy-start.7
  9.1 0.7 copy-done.7
  9.8 0.0 copy-start.8
  9.8 0.7 copy-done.8
  10.5 0.0 slice-start.1
  10.5 0.0 copy-start.9
  10.5 37.0 %qkv_rs.1.qkv = bf16[3,10,16,128]{3,2,1,0:T(8,128)(2,1)S(1)} custom-call(bf16[64,1280]{1,0:T(8,128)(2,1)S(1)} %copy-done.5, bf16[1,1280]{1,0:T(2,128)(2,1)S(1)} %reshape.15.gain, bf16[10,1280,128]{2,1,0:T(8,128)(2,1)S(1)} %bitcast.13, bf16[10,1280,128]{2,1,0:T(8,128)(2,1)S(1)} %bitcast.14, bf16[10,1280,128]{2,1,0:T(8,128)(2,1)S(1)} %bitcast.15, ...), custom_call_target="tpu_custom_call" | custom-call | flops 629145600 | bytes 80000000 | tf_op jit(solution)/shard_map/qkv_rs/pallas_call | solution.py:156
  47.5 0.0 slice-done
  47.5 0.0 slice-done.1
  47.5 0.0 copy-done.9
  47.5 0.0 copy-start
  47.5 2.5 %copy-done = bf16[16,128,10,128]{3,1,2,0:T(8,128)(2,1)S(1)} copy-done((bf16[16,128,10,128]{3,1,2,0:T(8,128)(2,1)S(1)}, bf16[16,128,10,128]{3,1,2,0:T(8,128)(2,1)}, u32[]{:S(2)}) %copy-start) | copy-done | bytes 5242904
  50.0 0.0 copy-start.1
  50.0 0.0 copy-start.6
  50.0 12.9 %attn.1 = (bf16[10,16,128]{2,1,0:T(8,128)(2,1)S(1)}, bf16[16,10,128,128]{3,2,1,0:T(8,128)(2,1)}, bf16[16,10,128,128]{3,2,1,0:T(8,128)(2,1)}) custom-call(s32[16]{0:T(128)S(1)} %copy-done.9, bf16[3,10,16,128]{3,2,1,0:T(8,128)(2,1)S(1)} %qkv_rs.1.qkv, bf16[16,10,128,128]{3,2,1,0:T(8,128)(2,1)S(1)} %bitcast.10, bf16[16,10,128,128]{3,2,1,0:T(8,128)(2,1)S(1)} %bitcast.11), custom_call_target="tpu_custom_call" | custom-call | flops 10485760 | bytes 20971520 | tf_op jit(solution)/shard_map/attn/pallas_call | solution.py:228
  62.9 0.0 copy-done.1
  62.9 0.0 copy-done.6
  62.9 68.2 %mlp.1 = bf16[64,1280]{1,0:T(8,128)(2,1)S(1)} custom-call(bf16[10,16,128]{2,1,0:T(8,128)(2,1)S(1)} %get-tuple-element.6.o_mine, bf16[64,1280]{1,0:T(8,128)(2,1)S(1)} %copy-done.6, bf16[1,1280]{1,0:T(2,128)(2,1)S(1)} %reshape.16.gain, bf16[1280,1280]{1,0:T(8,128)(2,1)S(1)} %bitcast.12, bf16[1280,3456]{1,0:T(8,128)(2,1)} %wg.1, bf16[1280,3456]{1,0:T(8,128)(2,1)} %wu.1, ...), custom_call_target="tpu_custom_call" | custom-call | flops 1908408320 | bytes 150000000 | tf_op jit(solution)/shard_map/mlp/pallas_call | solution.py:457
  131.1 0.7 copy.19
  (1 shorter events, 0.0 us)
Async XLA Ops:
  0.6 46.9 %slice-start = ((s8[5242880]{0:T(1024)(128)(4,1)}), s8[4194304]{0:T(1024)(128)(4,1)S(1)}, s32[]{:S(2)}) async-start(s8[5242880]{0:T(1024)(128)(4,1)} %bitcast.8), calls=%async_computation | async-start | bytes 8388608
  2.4 1.9 %copy-start.2 = (bf16[1280,10,128]{2,0,1:T(8,128)(2,1)S(1)}, bf16[1280,10,128]{2,0,1:T(8,128)(2,1)}, u32[]{:S(2)}) copy-start(bf16[1280,10,128]{2,0,1:T(8,128)(2,1)} %param.16) | copy-start | bytes 9830404
  4.3 1.9 %copy-start.3 = (bf16[1280,10,128]{2,0,1:T(8,128)(2,1)S(1)}, bf16[1280,10,128]{2,0,1:T(8,128)(2,1)}, u32[]{:S(2)}) copy-start(bf16[1280,10,128]{2,0,1:T(8,128)(2,1)} %param.17) | copy-start | bytes 9830404
  6.2 1.9 %copy-start.4 = (bf16[1280,10,128]{2,0,1:T(8,128)(2,1)S(1)}, bf16[1280,10,128]{2,0,1:T(8,128)(2,1)}, u32[]{:S(2)}) copy-start(bf16[1280,10,128]{2,0,1:T(8,128)(2,1)} %param.18) | copy-start | bytes 9830404
  8.1 0.9 copy-start.5
  9.1 0.7 copy-start.7
  9.8 0.7 copy-start.8
  10.5 37.1 %slice-start.1 = ((s8[5242880]{0:T(1024)(128)(4,1)}), s8[1048576]{0:T(1024)(128)(4,1)S(1)}, s32[]{:S(2)}) async-start(s8[5242880]{0:T(1024)(128)(4,1)} %bitcast.8), calls=%async_computation.1 | async-start | bytes 2097152
  10.5 37.1 %copy-start.9 = (s32[16]{0:T(128)S(1)}, s32[16]{0:T(128)}, u32[]{:S(2)}) copy-start(s32[16]{0:T(128)} %lens.1) | copy-start | bytes 196
  47.5 2.5 %copy-start = (bf16[16,128,10,128]{3,1,2,0:T(8,128)(2,1)S(1)}, bf16[16,128,10,128]{3,1,2,0:T(8,128)(2,1)}, u32[]{:S(2)}) copy-start(bf16[16,128,10,128]{3,1,2,0:T(8,128)(2,1)} %param.26) | copy-start | bytes 15728644
  50.0 12.9 %copy-start.1 = (bf16[10,128,1280]{2,1,0:T(8,128)(2,1)S(1)}, bf16[10,128,1280]{2,1,0:T(8,128)(2,1)}, u32[]{:S(2)}) copy-start(bf16[10,128,1280]{2,1,0:T(8,128)(2,1)} %param.19) | copy-start | bytes 9830404
  50.0 12.9 %copy-start.6 = (bf16[64,1280]{1,0:T(8,128)(2,1)S(1)}, bf16[64,1280]{1,0:T(8,128)(2,1)}, u32[]{:S(2)}) copy-start(bf16[64,1280]{1,0:T(8,128)(2,1)} %hid.3) | copy-start | bytes 491524

commit v2 on v0

v2 whole, which is shorter than its diff:
```python
import jax
import jax.numpy as jnp
from jax import lax
from jax.experimental import pallas as pl
from jax.experimental.pallas import tpu as pltpu
from jax.sharding import PartitionSpec as P

EPS = 1e-6
MESH = pl.DeviceIdType.MESH
F32 = jnp.float32
BF16 = jnp.bfloat16
NZ = 4
A_LAG = 2
E_LAG = 4
COL = 128
RCOL = 256


def remote(src, dst, send_sem, recv_sem, **where):
    return pltpu.make_async_remote_copy(src_ref=src, dst_ref=dst, send_sem=send_sem, recv_sem=recv_sem, device_id=where, device_id_type=MESH)


def partner(tp, k):
    if k == 1:
        return tp + 1 - 2 * lax.rem(tp, 2)
    return lax.rem(tp + 2, 4)


def pack_rows(col):
    rows = col.shape[0]
    lane = lax.broadcasted_iota(jnp.int32, (rows, 128), 1)
    row = lax.broadcasted_iota(jnp.int32, (rows, 128), 0)
    packed = jnp.sum(jnp.where(lane == row, col, 0.0), axis=0, keepdims=True)
    return jnp.broadcast_to(packed, (8, 128))


def unpack_rows(tile, rows):
    lane = lax.broadcasted_iota(jnp.int32, (rows, 128), 1)
    row = lax.broadcasted_iota(jnp.int32, (rows, 128), 0)
    wide = jnp.broadcast_to(tile[0:1], (rows, 128))
    return jnp.sum(jnp.where(lane == row, wide, 0.0), axis=1, keepdims=True)


def layer_kernel(hid_h, g1_h, g2_h, wq, wk, wv, wo, wg, wu, wd, kc, vc, lens_h, cos_h, sin_h,
                 out, k_out, v_out,
                 hid, g1, g2, lens, cos, sin, wbuf, wo_b, wg_b, wu_b, wd_b,
                 part, rbuf, lbuf, x_buf, o_x, new_kv, red, r1, s_buf, r2, h_mid, pbuf, rbuf2, lbuf2, mbuf,
                 cum_in, cum_out, own_sq, fac,
                 s_sem, w_sem, c_sem, b_sem, g_sem, rs, rr, ls, lr, o_s, o_r, a_s, a_r, b_s, b_r, c_s, c_r,
                 q_s, q_r, rs2, rr2, ls2, lr2, mr_s, mr_r, ml_s, ml_r):
    z = lax.axis_index('dm')
    tp = lax.axis_index('tp')
    rows, width = hid.shape
    full = width * NZ
    heads = wq.shape[0]
    hd = wq.shape[2]
    per = rows // NZ
    half = rows // 2
    slots = kc.shape[2]
    ff = wg.shape[1]
    n_col = ff // COL
    n_grp = g_sem.shape[1]
    grp = ff // n_grp
    n_red = width // RCOL
    early = (n_col * 2 // 3) // 2 * 2
    core = lax.rem(tp, 2)
    sib, across = partner(tp, 1), partner(tp, 2)
    nxt, prv = lax.rem(z + 1, NZ), lax.rem(z + NZ - 1, NZ)

    small = [pltpu.make_async_copy(a, b, s_sem.at[i]) for i, (a, b) in enumerate(((hid_h, hid), (g1_h, g1), (g2_h, g2), (cos_h, cos), (sin_h, sin), (lens_h, lens)))]
    load_o = pltpu.make_async_copy(wo, wo_b, b_sem.at[0])
    load_d = pltpu.make_async_copy(wd, wd_b, b_sem.at[1])

    def load_w(i, h):
        return pltpu.make_async_copy((wq, wk, wv)[i].at[h], wbuf.at[i, h], w_sem.at[i, h])

    def load_c(i, h):
        return pltpu.make_async_copy((kc, vc)[i].at[:, h], (k_out, v_out)[i].at[:, h], c_sem.at[i, h])

    def load(i, g):
        src, dst = ((wg, wg_b), (wu, wu_b))[i]
        cols = pl.ds(pl.multiple_of(g * grp, COL), grp)
        return pltpu.make_async_copy(src.at[:, cols], dst.at[:, cols], g_sem.at[i, g])

    for cp in small:
        cp.start()
    for h in range(heads):
        for i in range(3):
            load_w(i, h).start()
        if h >= 2:
            load_c(0, h - 2).start()
            load_c(1, h - 2).start()
    for h in range(max(heads - 2, 0), heads):
        load_c(0, h).start()
        load_c(1, h).start()
    load_o.start()
    for g in range(n_grp):
        load(0, g).start()
        load(1, g).start()
    load_d.start()

    sem = pltpu.get_barrier_semaphore()
    for k in range(1, NZ):
        pl.semaphore_signal(sem, inc=1, device_id={'dm': lax.rem(z + k, NZ)}, device_id_type=MESH)
    for k in (1, 2):
        pl.semaphore_signal(sem, inc=1, device_id={'tp': partner(tp, k)}, device_id_type=MESH)

    for cp in small:
        cp.wait()

    def local_norm(x, gain, step):
        col = jnp.sum(x * x, axis=-1, keepdims=True)
        own_sq[step] = pack_rows(col)
        x_buf[...] = (x * lax.rsqrt(col / full + EPS) * gain).astype(BF16)

    def inv(tile):
        return lax.rsqrt(tile / full + EPS)

    def stat(step, side):
        return remote(cum_out.at[step, side], cum_in.at[step, side], q_s.at[step, side], q_r.at[step, side], dm=(nxt, prv)[side])

    def relay_stat(step, side):
        has_in = (z > 0) if side == 0 else (z < NZ - 1)
        has_out = (z < NZ - 1) if side == 0 else (z > 0)

        @pl.when(has_in)
        def _():
            stat(step, side).wait_recv()

        @pl.when(jnp.logical_not(has_in))
        def _():
            cum_in[step, side] = jnp.zeros((8, 128), F32)

        before, own = cum_in[step, side], own_sq[step]
        cum = before + own
        cum_out[step, side] = cum

        @pl.when(has_out)
        def _():
            stat(step, side).start()

        scale = inv(cum)
        put_fac(2 * side, scale / inv(own))
        put_fac(2 * side + 1, scale / inv(before))

    def put_fac(i, tile):
        wide = jnp.broadcast_to(unpack_rows(tile, rows), (rows, 128))
        for d in range(NZ):
            fac[i, d] = wide[d * per:(d + 1) * per]

    local_norm(hid[...].astype(F32), g1[...].astype(F32).reshape(1, width), 0)
    cos2 = jnp.concatenate([cos[...], cos[...]], axis=-1)
    sin2 = jnp.concatenate([-sin[...], sin[...]], axis=-1)

    @pl.when(z == 0)
    def _():
        rbuf[0] = jnp.zeros(rbuf.shape[1:], F32)

    @pl.when(z == NZ - 1)
    def _():
        lbuf[NZ - 1] = jnp.zeros(lbuf.shape[1:], F32)

    row = lax.broadcasted_iota(jnp.int32, (per, slots), 0)
    pos = lax.broadcasted_iota(jnp.int32, (per, slots), 1)
    length = jnp.zeros((per, slots), jnp.int32)
    for r in range(per):
        length = jnp.where(row == r, lens[r], length)
    at_len = pos == length
    seen = pos <= length

    pl.semaphore_wait(sem, NZ + 1)

    def right(d, p):
        return remote(part.at[d, p], rbuf.at[d, p], rs.at[d, p], rr.at[d, p], dm=nxt)

    def left(d, p):
        return remote(part.at[d, p], lbuf.at[d, p], ls.at[d, p], lr.at[d, p], dm=prv)

    def o_view(src, p):
        return o_x.at[pl.ds(pl.multiple_of(src * per, per), per), pl.ds(pl.multiple_of(p * hd, hd), hd)]

    def o_copy(src, to, p):
        return remote(o_view(src, p), o_view(src, p), o_s.at[p, to], o_r.at[p, src], dm=to)

    def thrice(i, d):
        f = fac[i, d]
        return jnp.concatenate([f, f, f], axis=1)

    def attend(h):
        y = part[z, h] * thrice(4, z) + (rbuf[z, h] * thrice(5, z) + lbuf[z, h] * thrice(6, z))
        q, k = y[:, 0:hd], y[:, hd:2 * hd]
        q = (q * cos2 + pltpu.roll(q, hd // 2, 1) * sin2).astype(BF16)
        k_new = (k * cos2 + pltpu.roll(k, hd // 2, 1) * sin2).astype(BF16).astype(F32)
        v_new = y[:, 2 * hd:].astype(BF16).astype(F32)
        new_kv[0, h] = k_new
        new_kv[1, h] = v_new
        load_c(0, h).wait()
        load_c(1, h).wait()
        s = jnp.zeros((per, slots), F32)
        for r in range(per):
            t = lax.dot_general(q, k_out[r, h], (((1,), (1,)), ((), ())), preferred_element_type=F32)
            s = jnp.where(row == r, t, s)
        s_new = jnp.sum(q.astype(F32) * k_new, axis=-1, keepdims=True)
        s = jnp.where(at_len, s_new, s) * (hd ** -0.5)
        s = jnp.where(seen, s, -1e30)
        e = jnp.exp(s - jnp.max(s, axis=-1, keepdims=True))
        prob = (e / jnp.sum(e, axis=-1, keepdims=True)).astype(BF16).astype(F32)
        p_new = jnp.sum(jnp.where(at_len, prob, 0.0), axis=-1, keepdims=True)
        p_old = jnp.where(at_len, 0.0, prob).astype(BF16)
        acc = jnp.zeros((per, hd), F32)
        for r in range(per):
            t = jnp.dot(p_old, v_out[r, h], preferred_element_type=F32)
            acc = jnp.where(row == r, t, acc)
        o_x[pl.ds(pl.multiple_of(z * per, per), per), pl.ds(pl.multiple_of(h * hd, hd), hd)] = (acc + p_new * v_new).astype(BF16)
        for k in (2, 1, 3):
            o_copy(z, lax.rem(z + k, NZ), h).start()

    def patch(lo, hi):
        where = lax.broadcasted_iota(jnp.int32, (slots, hd), 0)

        def body(h, carry):
            for r in range(per):
                hit = where == lens[r]
                for i, ref in enumerate((k_out, v_out)):
                    fresh = jnp.broadcast_to(new_kv[i, h, r:r + 1, :], (slots, hd))
                    ref[r, h] = jnp.where(hit, fresh, ref[r, h].astype(F32)).astype(BF16)
            return carry

        lax.fori_loop(lo, hi, body, 0)

    def a_slot(t, carry):
        @pl.when(t < heads)
        def _():
            for i in range(3):
                load_w(i, t).wait()
                y = jnp.dot(x_buf[...], wbuf[i, t], preferred_element_type=F32)
                for d in range(NZ):
                    part[d, t, :, i * hd:(i + 1) * hd] = y[d * per:(d + 1) * per]

        p = t - A_LAG * z

        @pl.when(p == 0)
        def _():
            relay_stat(0, 0)

        @pl.when((p >= 0) & (p < heads))
        def _():
            for d in (3, 2, 1):
                @pl.when((z > 0) & (z <= d))
                def _(d=d):
                    right(d, p).wait_recv()

                @pl.when((z > 0) & (z < d))
                def _(d=d):
                    part[d, p] = part[d, p] * thrice(0, d) + rbuf[d, p] * thrice(1, d)

                @pl.when(z < d)
                def _(d=d):
                    right(d, p).start()

        b = t - A_LAG * (NZ - 1 - z)

        @pl.when(b == 0)
        def _():
            relay_stat(0, 1)

        @pl.when((b >= 0) & (b < heads))
        def _():
            for d in (0, 1, 2):
                @pl.when((z < NZ - 1) & (z >= d))
                def _(d=d):
                    left(d, b).wait_recv()

                @pl.when((z < NZ - 1) & (z > d))
                def _(d=d):
                    part[d, b] = part[d, b] * thrice(2, d) + lbuf[d, b] * thrice(3, d)

                @pl.when(z > d)
                def _(d=d):
                    left(d, b).start()

        f = t - A_LAG * jnp.maximum(z, NZ - 1 - z)

        @pl.when(f == 0)
        def _():
            own = own_sq[0]
            scale = inv((cum_in[0, 0] + own) + cum_in[0, 1])
            put_fac(4, scale / inv(own))
            put_fac(5, scale / inv(cum_in[0, 0]))
            put_fac(6, scale / inv(cum_in[0, 1]))

        @pl.when((f >= 0) & (f < heads))
        def _():
            attend(f)

        return carry

    lax.fori_loop(0, heads + A_LAG * (NZ - 1), a_slot, 0)
    patch(0, heads // 2)

    def o_wait(p, carry):
        for k in (1, 3, 2):
            o_copy(lax.rem(z + k, NZ), lax.rem(z + k, NZ), p).wait_recv()
        return carry

    lax.fori_loop(0, heads, o_wait, 0)
    load_o.wait()

    mine = pl.ds(pl.multiple_of(core * half, half), half)
    other = pl.ds(pl.multiple_of((1 - core) * half, half), half)

    def reduce_tp(step, product, base, dst, meanwhile):
        def a_copy(j):
            return remote(red.at[j, other], r1.at[step, j], a_s.at[step, j], a_r.at[step, j], tp=sib)

        def b_copy(j):
            return remote(s_buf.at[step, j], r2.at[step, j], b_s.at[step, j], b_r.at[step, j], tp=across)

        def c_copy(j, part_rows):
            view = dst.at[part_rows, pl.ds(j * RCOL, RCOL)]
            return remote(view, view, c_s.at[step, j], c_r.at[step, j], tp=sib)

        for j in range(n_red):
            red[j] = product(j)
            a_copy(j).start()
        for j in range(n_red):
            a_copy(j).wait_recv()
            s_buf[step, j] = red[j, mine] + r1[step, j]
            b_copy(j).start()
        meanwhile()
        for j in range(n_red):
            b_copy(j).wait_recv()
            total = (s_buf[step, j] + r2[step, j]).astype(BF16)
            cols = pl.ds(j * RCOL, RCOL)
            dst[mine, cols] = (base[mine, cols].astype(F32) + total.astype(F32)).astype(BF16)
            c_copy(j, mine).start()
        for j in range(n_red):
            c_copy(j, other).wait_recv()
        for j in range(n_red):
            a_copy(j).wait_send()
            b_copy(j).wait_send()
            c_copy(j, mine).wait_send()

    reduce_tp(0, lambda j: jnp.dot(o_x[...], wo_b[:, j * RCOL:(j + 1) * RCOL], preferred_element_type=F32), hid, h_mid, lambda: patch(heads // 2, heads))
    local_norm(h_mid[...].astype(F32), g2[...].astype(F32).reshape(1, width), 1)

    def right2(c):
        return remote(pbuf.at[c, 1], rbuf2.at[c], rs2.at[c], rr2.at[c], dm=nxt)

    def left2(c):
        return remote(pbuf.at[c, 0], lbuf2.at[c], ls2.at[c], lr2.at[c], dm=prv)

    low, high = pl.ds(0, half), pl.ds(half, half)

    def cols_of(c):
        return pl.ds(pl.multiple_of(c * COL, COL), COL)

    def m_left(c):
        view = mbuf.at[high, cols_of(c)]
        return remote(view, view, mr_s.at[c], mr_r.at[c], dm=prv)

    def m_right(c):
        view = mbuf.at[low, cols_of(c)]
        return remote(view, view, ml_s.at[c], ml_r.at[c], dm=nxt)

    def gated(a):
        g, u = a[:, :COL], a[:, COL:]
        return (g * (1.0 / (1.0 + jnp.exp(-g))) * u).astype(BF16)

    def wide(i, first):
        f = jnp.concatenate([fac[i, first], fac[i, first + 1]], axis=0)
        return jnp.concatenate([f, f], axis=1)

    def e_slot(t, carry):
        @pl.when(t < n_col)
        def _():
            per_grp = n_col // n_grp

            @pl.when(lax.rem(t, per_grp) == 0)
            def _():
                load(0, t // per_grp).wait()
                load(1, t // per_grp).wait()

            g = jnp.dot(x_buf[...], wg_b[:, cols_of(t)], preferred_element_type=F32)
            u = jnp.dot(x_buf[...], wu_b[:, cols_of(t)], preferred_element_type=F32)
            pbuf[t, 0, :, 0:COL] = g[:half]
            pbuf[t, 1, :, 0:COL] = g[half:]
            pbuf[t, 0, :, COL:] = u[:half]
            pbuf[t, 1, :, COL:] = u[half:]

        c = t - E_LAG * z

        @pl.when(c == 0)
        def _():
            relay_stat(1, 0)

        @pl.when((c >= 0) & (c < n_col))
        def _():
            @pl.when(z > 0)
            def _():
                right2(c).wait_recv()
                pbuf[c, 1] = pbuf[c, 1] * wide(0, 2) + rbuf2[c] * wide(1, 2)

            @pl.when(z < NZ - 1)
            def _():
                right2(c).start()

            @pl.when(z == NZ - 1)
            def _():
                mbuf[high, cols_of(c)] = gated(pbuf[c, 1])
                m_left(c).start()

        b = t - E_LAG * (NZ - 1 - z)

        @pl.when(b == 0)
        def _():
            relay_stat(1, 1)

        @pl.when((b >= 0) & (b < n_col))
        def _():
            @pl.when(z < NZ - 1)
            def _():
                left2(b).wait_recv()
                pbuf[b, 0] = pbuf[b, 0] * wide(2, 0) + lbuf2[b] * wide(3, 0)

            @pl.when(z > 0)
            def _():
                left2(b).start()

            @pl.when(z == 0)
            def _():
                mbuf[low, cols_of(b)] = gated(pbuf[b, 0])
                m_right(b).start()

        e = t - E_LAG * (2 * NZ - 2 - z)

        @pl.when((e >= 0) & (e < n_col) & (z < NZ - 1))
        def _():
            m_left(e).wait_recv()

            @pl.when(z > 0)
            def _():
                m_left(e).start()

        f = t - E_LAG * (NZ - 1 + z)

        @pl.when((f >= 0) & (f < n_col) & (z > 0))
        def _():
            m_right(f).wait_recv()

            @pl.when(z < NZ - 1)
            def _():
                m_right(f).start()

        w = t - (early + E_LAG * (2 * NZ - 2))

        @pl.when(w == 0)
        def _():
            load_d.wait()

        @pl.when((w >= 0) & (w < n_red))
        def _():
            red[w] = jnp.dot(mbuf[:, 0:early * COL], wd_b[0:early * COL, pl.ds(pl.multiple_of(w * RCOL, RCOL), RCOL)], preferred_element_type=F32)

        return carry

    lax.fori_loop(0, max(n_col, early + n_red) + E_LAG * (2 * NZ - 2), e_slot, 0)
    reduce_tp(1, lambda j: red[j] + jnp.dot(mbuf[:, early * COL:], wd_b[early * COL:, j * RCOL:(j + 1) * RCOL], preferred_element_type=F32), h_mid, out, lambda: None)

    def drain_a(p, carry):
        for d in range(NZ):
            @pl.when(z < d)
            def _(d=d):
                right(d, p).wait_send()

            @pl.when(z > d)
            def _(d=d):
                left(d, p).wait_send()

        for k in range(1, NZ):
            o_copy(z, lax.rem(z + k, NZ), p).wait_send()
        return carry

    lax.fori_loop(0, heads, drain_a, 0)

    def drain_e(c, carry):
        @pl.when(z < NZ - 1)
        def _():
            right2(c).wait_send()
            m_right(c).wait_send()

        @pl.when(z > 0)
        def _():
            left2(c).wait_send()
            m_left(c).wait_send()

        return carry

    lax.fori_loop(0, n_col, drain_e, 0)
    for step in range(2):
        @pl.when(z < NZ - 1)
        def _(step=step):
            stat(step, 0).wait_send()

        @pl.when(z > 0)
        def _(step=step):
            stat(step, 1).wait_send()


def layer_call(hid, g1, g2, wq, wk, wv, wo, wg, wu, wd, kc, vc, lens, cos, sin):
    rows, width = hid.shape
    heads, hd = wq.shape[0], wq.shape[2]
    ff = wg.shape[1]
    per, half = rows // NZ, rows // 2
    n_col, n_red = ff // COL, width // RCOL
    n_grp = 9 if n_col % 9 == 0 else 1
    vm = pl.BlockSpec(memory_space=pltpu.VMEM)
    hbm = pl.BlockSpec(memory_space=pl.ANY)
    dma = pltpu.SemaphoreType.DMA
    lane_sum = pltpu.VMEM((NZ, heads, per, 3 * hd), F32)
    red = pltpu.VMEM((2, n_red, half, RCOL), F32)
    act = pltpu.VMEM((rows, width), BF16)
    return pl.pallas_call(
        layer_kernel,
        name='layer',
        out_shape=[pltpu.VMEM((rows, width), BF16), pltpu.VMEM(kc.shape, BF16), pltpu.VMEM(vc.shape, BF16)],
        in_specs=[hbm] * 15,
        out_specs=[vm, vm, vm],
        scratch_shapes=[
            act, pltpu.VMEM(g1.shape, g1.dtype), pltpu.VMEM(g2.shape, g2.dtype), pltpu.SMEM(lens.shape, jnp.int32), pltpu.VMEM(cos.shape, F32), pltpu.VMEM(sin.shape, F32),
            pltpu.VMEM((3, heads, width, hd), BF16),
            pltpu.VMEM(wo.shape, BF16), pltpu.VMEM(wg.shape, BF16), pltpu.VMEM(wu.shape, BF16), pltpu.VMEM(wd.shape, BF16),
            lane_sum, lane_sum, lane_sum,
            act, act,
            pltpu.VMEM((2, heads, per, hd), F32),
            pltpu.VMEM((n_red, rows, RCOL), F32),
            red, red, red,
            act,
            pltpu.VMEM((n_col, 2, half, 2 * COL), F32),
            pltpu.VMEM((n_col, half, 2 * COL), F32),
            pltpu.VMEM((n_col, half, 2 * COL), F32),
            pltpu.VMEM((rows, ff), BF16),
            pltpu.VMEM((2, 2, 8, 128), F32), pltpu.VMEM((2, 2, 8, 128), F32), pltpu.VMEM((2, 8, 128), F32),
            pltpu.VMEM((7, NZ, per, 128), F32),
            dma((6,)), dma((3, heads)), dma((2, heads)), dma((2,)), dma((2, n_grp)),
            dma((NZ, heads)), dma((NZ, heads)), dma((NZ, heads)), dma((NZ, heads)),
            dma((heads, NZ)), dma((heads, NZ)),
            dma((2, n_red)), dma((2, n_red)), dma((2, n_red)), dma((2, n_red)), dma((2, n_red)), dma((2, n_red)),
            dma((2, 2)), dma((2, 2)),
            dma((n_col,)), dma((n_col,)), dma((n_col,)), dma((n_col,)),
            dma((n_col,)), dma((n_col,)), dma((n_col,)), dma((n_col,)),
        ],
        compiler_params=pltpu.CompilerParams(collective_id=0, has_side_effects=True, vmem_limit_bytes=VMEM_KIB * 1024),
    )(hid, g1, g2, wq, wk, wv, wo, wg, wu, wd, kc, vc, lens, cos, sin)


VMEM_KIB = 49 * 1024


def solution(mesh):
    row_spec = P('dp', 'dm')
    cache_spec = P(('dp', 'dm'), None, 'tp', None)
    batch_spec = P(('dp', 'dm'))
    rope_spec = P(('dp', 'dm'), None)
    in_specs = (row_spec, P('dm', 'tp', None), P('dm', 'tp', None), P('dm', 'tp', None), P('tp', None, 'dm'), P('dm', 'tp'), P('dm', 'tp'), P('tp', 'dm'), P('dm'), P('dm'), cache_spec, cache_spec, batch_spec, rope_spec, rope_spec)
    out_specs = (row_spec, cache_spec, cache_spec)

    def local_layer(hidden, w_q, w_k, w_v, w_o, w_gate, w_up, w_down, norm_attn, norm_mlp, k_cache, v_cache, seq_lens, rope_cos, rope_sin):
        by_head = [w.transpose(1, 0, 2) for w in (w_q, w_k, w_v)]
        caches = [c.transpose(0, 2, 1, 3) for c in (k_cache, v_cache)]
        h_out, k_out, v_out = layer_call(hidden, norm_attn, norm_mlp, *by_head, w_o.reshape(-1, w_o.shape[-1]), w_gate, w_up, w_down, *caches, seq_lens, rope_cos, rope_sin)
        return h_out, k_out.transpose(0, 2, 1, 3), v_out.transpose(0, 2, 1, 3)

    return jax.shard_map(local_layer, mesh=mesh, in_specs=in_specs, out_specs=out_specs, check_vma=False)
```

time: 262 us -> 110 us (0.42)
  waiting for transfers between devices: 129 us -> 0 us
  Pallas kernels: 0 us -> 104 us
  blocking collectives: 64.8 us -> 0 us
  matrix products: 37.4 us -> 0 us
  between operations: 13.9 us -> 0.65 us
  other arithmetic: 13.1 us -> 0 us
  local copies, waits for them, and re-layouts: 2.44 us -> 5.38 us
    pallas_call x0 -> x1, Pallas kernels: none -> 104 us  [layer_call(): pl.pallas_call(layer_kernel, name='layer', out_shape=[pltpu.VMEM((rows, w...]
    psum x1 -> x0, waiting for transfers between devices: 75.1 us -> none  [local_layer(): lax.psum(jnp.dot(x_mlp, w_up, preferred_element_type=jnp.float32), 'dm')]
    reduce_scatter x3 -> x0, waiting for transfers between devices: 54.1 us -> none  [the longest x1 21.7 us: local_layer(): q_rows = lax.psum_scatter(q_part, 'dm', scatter_dimension=0, tiled=True)]
    psum x4 -> x0, blocking collectives: 51.3 us -> none  [the longest x2 22.2 us: width_norm(): sq_sum = lax.psum(jnp.sum(x_f32 * x_f32, axis=-1, keepdims=True), 'dm')]
    dot_general x9 -> x0, matrix products: 37.4 us -> none  [the longest x1 6.43 us: local_layer(): jnp.dot(gated_act, w_down, preferred_element_type=jnp.float32)]
    all_gather x1 -> x0, blocking collectives: 13.5 us -> none  [local_layer(): heads_all = lax.all_gather(attn_heads, 'dm', axis=0, tiled=True)]
    select_n x1 -> x0, other arithmetic: 6.92 us -> none  [attend(): k_out = jnp.where(write_mask, k_rot[:, None], k_cache)]
    unnamed x18 -> x3, local copies, waits for them, and re-layouts: 2.4 us -> 5.38 us
  transfers between devices with their start and end apart: 4 -> 0, of which waited for: 4 -> 0; matrix products, arithmetic and copies ran while one was open for 3% -> 0% of each run, Pallas kernels for 0% -> 0%
where the time goes in v2:
time: 110 us
  Pallas kernels  104 us (95%)
  local copies, waits for them, and re-layouts  5.38 us (5%)
    pallas_call x1, Pallas kernels, layer_call(): pl.pallas_call(layer_kernel, name='layer', out_shape=[pltpu.VMEM((rows, w...  104 us
    unnamed x3, local copies, waits for them, and re-layouts  5.38 us

profile of v2, /device:TPU:0, one launch (start us, length us, event | category | flops | bytes accessed | tf_op | source)
XLA Modules:
  0.0 110.2 jit_solution(10160756925060683885)
XLA Ops:
  0.6 104.2 %layer.1 = (bf16[64,1280]{1,0:T(8,128)(2,1)S(1)}, bf16[16,10,128,128]{3,2,1,0:T(8,128)(2,1)S(1)}, bf16[16,10,128,128]{3,2,1,0:T(8,128)(2,1)S(1)}) custom-call(bf16[64,1280]{1,0:T(8,128)(2,1)} %hid_h.1, bf16[1280]{0:T(1024)(128)(2,1)} %g1_h.1, bf16[1280]{0:T(1024)(128)(2,1)} %g2_h.1, bf16[10,1280,128]{2,1,0:T(8,128)(2,1)} %bitcast.12, ...), custom_call_target="tpu_custom_call" | custom-call | tf_op jit(solution)/shard_map/layer/pallas_call | solution.py:523
  104.9 0.7 copy.21
  105.5 2.4 %copy.22 = bf16[16,128,10,128]{3,1,2,0:T(8,128)(2,1)} copy(bf16[16,128,10,128]{3,1,2,0:T(8,128)(2,1)S(1)} %bitcast.9) | data formatting | bytes 10485760
  107.9 2.4 %copy.23 = bf16[16,128,10,128]{3,1,2,0:T(8,128)(2,1)} copy(bf16[16,128,10,128]{3,1,2,0:T(8,128)(2,1)S(1)} %bitcast.8) | data formatting | bytes 10485760

commit v3 on v2

--- a/solution.py
+++ b/solution.py
@@ -11,8 +11,8 @@
 BF16 = jnp.bfloat16
 NZ = 4
 A_LAG = 2
-E_LAG = 4
-COL = 128
+E_LAG = 2
+COL = 384
 RCOL = 256
 
 
@@ -369,7 +369,7 @@
 
     def wide(i, first):
         f = jnp.concatenate([fac[i, first], fac[i, first + 1]], axis=0)
-        return jnp.concatenate([f, f], axis=1)
+        return jnp.concatenate([f] * (2 * COL // 128), axis=1)
 
     def e_slot(t, carry):
         @pl.when(t < n_col)

time: 110 us -> 111 us (level)
  no operation moved by 1% of the time
where the time goes in v3:
time: 111 us
  Pallas kernels  105 us (95%)
  local copies, waits for them, and re-layouts  5.38 us (5%)
    pallas_call x1, Pallas kernels, layer_call(): pl.pallas_call(layer_kernel, name='layer', out_shape=[pltpu.VMEM((rows, w...  105 us
    unnamed x3, local copies, waits for them, and re-layouts  5.38 us

profile of v3, /device:TPU:0, one launch (start us, length us, event | category | flops | bytes accessed | tf_op | source)
XLA Modules:
  0.0 111.2 jit_solution(18085086369744813604)
XLA Ops:
  0.6 105.2 %layer.1 = (bf16[64,1280]{1,0:T(8,128)(2,1)S(1)}, bf16[16,10,128,128]{3,2,1,0:T(8,128)(2,1)S(1)}, bf16[16,10,128,128]{3,2,1,0:T(8,128)(2,1)S(1)}) custom-call(bf16[64,1280]{1,0:T(8,128)(2,1)} %hid_h.1, bf16[1280]{0:T(1024)(128)(2,1)} %g1_h.1, bf16[1280]{0:T(1024)(128)(2,1)} %g2_h.1, bf16[10,1280,128]{2,1,0:T(8,128)(2,1)} %bitcast.12, ...), custom_call_target="tpu_custom_call" | custom-call | tf_op jit(solution)/shard_map/layer/pallas_call | solution.py:523
  105.8 0.7 copy.21
  106.5 2.4 %copy.22 = bf16[16,128,10,128]{3,1,2,0:T(8,128)(2,1)} copy(bf16[16,128,10,128]{3,1,2,0:T(8,128)(2,1)S(1)} %bitcast.9) | data formatting | bytes 10485760
  108.8 2.4 %copy.23 = bf16[16,128,10,128]{3,1,2,0:T(8,128)(2,1)} copy(bf16[16,128,10,128]{3,1,2,0:T(8,128)(2,1)S(1)} %bitcast.8) | data formatting | bytes 10485760

commit v4 on v3

v4 whole, which is shorter than its diff:
```python
import jax
import jax.numpy as jnp
from jax import lax
from jax.experimental import pallas as pl
from jax.experimental.pallas import tpu as pltpu
from jax.sharding import PartitionSpec as P

EPS = 1e-6
MESH = pl.DeviceIdType.MESH
F32 = jnp.float32
BF16 = jnp.bfloat16
NZ = 4
NP = 8
A_LAG = 2
E_LAG = 3
COL = 384
DIRECT = 4


def remote(src, dst, send_sem, recv_sem, **where):
    return pltpu.make_async_remote_copy(src_ref=src, dst_ref=dst, send_sem=send_sem, recv_sem=recv_sem, device_id=where, device_id_type=MESH)


def partner(tp, k):
    if k == 1:
        return tp + 1 - 2 * lax.rem(tp, 2)
    return lax.rem(tp + 2, 4)


def pack_rows(col):
    rows = col.shape[0]
    lane = lax.broadcasted_iota(jnp.int32, (rows, 128), 1)
    row = lax.broadcasted_iota(jnp.int32, (rows, 128), 0)
    packed = jnp.sum(jnp.where(lane == row, col, 0.0), axis=0, keepdims=True)
    return jnp.broadcast_to(packed, (8, 128))


def unpack_rows(tile, rows):
    lane = lax.broadcasted_iota(jnp.int32, (rows, 128), 1)
    row = lax.broadcasted_iota(jnp.int32, (rows, 128), 0)
    wide = jnp.broadcast_to(tile[0:1], (rows, 128))
    return jnp.sum(jnp.where(lane == row, wide, 0.0), axis=1, keepdims=True)


def layer_kernel(hid_h, g1_h, g2_h, wq, wk, wv, wo, wg, wu, wd, kc, vc, lens_h, cos_h, sin_h,
                 out, k_out, v_out,
                 hid, g1, g2, lens, cos, sin, hid_p, len_v, rope, wbuf, wo_b, wg_b, wu_b, wd_b,
                 part, rbuf, lbuf, x_buf, o_x, o_cat, new_kv, red, r1, s_buf, r2, h_mid, h_fin, pbuf, rbuf2, lbuf2, mbuf,
                 cum_in, cum_out, own_sq, fac,
                 s_sem, w_sem, c_sem, b_sem, g_sem, rs, rr, ls, lr, o_s, o_r, a_s, a_r, b_s, b_r, c_s, c_r,
                 q_s, q_r, rs2, rr2, ls2, lr2, mr_s, mr_r, ml_s, ml_r, far_s):
    z = lax.axis_index('dm')
    tp = lax.axis_index('tp')
    rows, width = hid.shape
    full = width * NZ
    heads = wq.shape[0]
    hd = wq.shape[2]
    per = rows // NZ
    half = rows // 2
    side = half // 2
    slots = kc.shape[2]
    ff = wg.shape[1]
    n_pair = heads // 2
    n_a = 2 * n_pair
    n_col = ff // COL
    second = max(n_col, 8)
    n_e = second + n_col
    trip = E_LAG * (NZ - 1)
    n_grp = g_sem.shape[1]
    n_red = red.shape[1]
    rcol = width // n_red
    early = n_col * 2 // 3
    direct_from = n_e - DIRECT
    core = lax.rem(tp, 2)
    sib, across = partner(tp, 1), partner(tp, 2)
    nxt, prv = lax.rem(z + 1, NZ), lax.rem(z + NZ - 1, NZ)

    small = [pltpu.make_async_copy(a, b, s_sem.at[i]) for i, (a, b) in enumerate(((hid_h, hid), (g1_h, g1), (g2_h, g2), (cos_h, cos), (sin_h, sin), (lens_h, lens)))]
    load_o = pltpu.make_async_copy(wo, wo_b, b_sem.at[0])
    load_d = pltpu.make_async_copy(wd, wd_b, b_sem.at[1])

    def load_w(i, h):
        return pltpu.make_async_copy((wq, wk, wv)[i].at[h], wbuf.at[i, h], w_sem.at[i, h])

    def load_c(i, h):
        return pltpu.make_async_copy((kc, vc)[i].at[:, h], (k_out, v_out)[i].at[:, h], c_sem.at[i, h])

    def load(i, g):
        src, dst = ((wg, wg_b), (wu, wu_b))[i]
        cols = pl.ds(pl.multiple_of(g * COL, COL), COL)
        return pltpu.make_async_copy(src.at[:, cols], dst.at[:, cols], g_sem.at[i, g])

    for cp in small:
        cp.start()
    for h in range(heads):
        for i in range(3):
            load_w(i, h).start()
        if h >= 2:
            load_c(0, h - 2).start()
            load_c(1, h - 2).start()
    for h in range(max(heads - 2, 0), heads):
        load_c(0, h).start()
        load_c(1, h).start()
    load_o.start()
    for g in range(n_grp):
        load(0, g).start()
        load(1, g).start()
    load_d.start()

    sem = pltpu.get_barrier_semaphore()
    for k in range(1, NZ):
        pl.semaphore_signal(sem, inc=1, device_id={'dm': lax.rem(z + k, NZ)}, device_id_type=MESH)
    for k in (1, 2):
        pl.semaphore_signal(sem, inc=1, device_id={'tp': partner(tp, k)}, device_id_type=MESH)

    for cp in small:
        cp.wait()

    def inv(tile):
        return lax.rsqrt(tile / full + EPS)

    def local_norm(x, gain, step, lo):
        col = jnp.sum(x * x, axis=-1, keepdims=True)
        own_sq[step] = pack_rows(col)
        x_buf[lo:lo + x.shape[0]] = (x * lax.rsqrt(col / full + EPS) * gain).astype(BF16)

    def place(b, d):
        return d * per + b * NP

    x0 = hid[...].astype(F32)
    x0 = jnp.concatenate([x0[place(b, d):place(b, d) + NP] for b in range(2) for d in range(NZ)], axis=0)
    hid_p[...] = x0.astype(BF16)
    local_norm(x0, g1[...].astype(F32).reshape(1, width), 0, 0)
    cs, sn = cos[...], sin[...]
    row = lax.broadcasted_iota(jnp.int32, (NP, slots), 0)
    pos = lax.broadcasted_iota(jnp.int32, (NP, slots), 1)
    for b in range(2):
        part_cs, part_sn = cs[b * NP:(b + 1) * NP], sn[b * NP:(b + 1) * NP]
        rope[0, b] = jnp.concatenate([part_cs, part_cs], axis=-1)
        rope[1, b] = jnp.concatenate([-part_sn, part_sn], axis=-1)
        length = jnp.zeros((NP, slots), jnp.int32)
        for r in range(NP):
            length = jnp.where(row == r, lens[b * NP + r], length)
        len_v[b] = length

    def stat(step, way):
        return remote(cum_out.at[step, way], cum_in.at[step, way], q_s.at[step, way], q_r.at[step, way], dm=(nxt, prv)[way])

    def put_fac(i, tile, halves):
        n = len(halves) * half
        wide = jnp.broadcast_to(unpack_rows(tile, n), (n, 128))
        for k, b in enumerate(halves):
            for d in range(NZ):
                lo = (k * NZ + d) * NP
                fac[i, b, d] = wide[lo:lo + NP]

    def relay_stat(step, way, halves):
        has_in = (z > 0) if way == 0 else (z < NZ - 1)
        has_out = (z < NZ - 1) if way == 0 else (z > 0)

        @pl.when(has_in)
        def _():
            stat(step, way).wait_recv()

        @pl.when(jnp.logical_not(has_in))
        def _():
            cum_in[step, way] = jnp.zeros((8, 128), F32)

        before, own = cum_in[step, way], own_sq[step]
        cum = before + own
        cum_out[step, way] = cum

        @pl.when(has_out)
        def _():
            stat(step, way).start()

        scale = inv(cum)
        put_fac(2 * way, scale / inv(own), halves)
        put_fac(2 * way + 1, scale / inv(before), halves)

    @pl.when(z == 0)
    def _():
        rbuf[0] = jnp.zeros(rbuf.shape[1:], F32)

    @pl.when(z == NZ - 1)
    def _():
        lbuf[NZ - 1] = jnp.zeros(lbuf.shape[1:], F32)

    pl.semaphore_wait(sem, NZ + 1)

    def right(d, p):
        return remote(part.at[d, p], rbuf.at[d, p], rs.at[d, p], rr.at[d, p], dm=nxt)

    def left(d, p):
        return remote(part.at[d, p], lbuf.at[d, p], ls.at[d, p], lr.at[d, p], dm=prv)

    def split(it):
        b = it // n_pair
        return b, it - b * n_pair

    def o_copy(src, to, it):
        b, p = split(it)
        view = o_x.at[b, src, pl.ds(2 * p, 2)]
        return remote(view, view, o_s.at[it, to], o_r.at[it, src], dm=to)

    def repeat(f, n):
        return jnp.concatenate([f] * n, axis=1)

    def attend(it):
        b, p = split(it)
        y6 = part[z, it] * repeat(fac[4, b, z], 6) + (rbuf[z, it] * repeat(fac[5, b, z], 6) + lbuf[z, it] * repeat(fac[6, b, z], 6))
        cos2, sin2 = rope[0, b], rope[1, b]
        at_len = pos == len_v[b]
        seen = pos <= len_v[b]
        for e in range(2):
            h = 2 * p + e
            y = y6[:, e * 3 * hd:(e + 1) * 3 * hd]
            q, k = y[:, 0:hd], y[:, hd:2 * hd]
            q = (q * cos2 + pltpu.roll(q, hd // 2, 1) * sin2).astype(BF16)
            k_new = (k * cos2 + pltpu.roll(k, hd // 2, 1) * sin2).astype(BF16).astype(F32)
            v_new = y[:, 2 * hd:].astype(BF16).astype(F32)
            new_kv[0, h, b] = k_new
            new_kv[1, h, b] = v_new

            @pl.when(b == 0)
            def _(h=h):
                load_c(0, h).wait()
                load_c(1, h).wait()

            s = jnp.zeros((NP, slots), F32)
            for r in range(NP):
                t = lax.dot_general(q, k_out[b * NP + r, h], (((1,), (1,)), ((), ())), preferred_element_type=F32)
                s = jnp.where(row == r, t, s)
            s_new = jnp.sum(q.astype(F32) * k_new, axis=-1, keepdims=True)
            s = jnp.where(at_len, s_new, s) * (hd ** -0.5)
            s = jnp.where(seen, s, -1e30)
            ex = jnp.exp(s - jnp.max(s, axis=-1, keepdims=True))
            prob = (ex / jnp.sum(ex, axis=-1, keepdims=True)).astype(BF16).astype(F32)
            p_new = jnp.sum(jnp.where(at_len, prob, 0.0), axis=-1, keepdims=True)
            p_old = jnp.where(at_len, 0.0, prob).astype(BF16)
            acc = jnp.zeros((NP, hd), F32)
            for r in range(NP):
                t = jnp.dot(p_old, v_out[b * NP + r, h], preferred_element_type=F32)
                acc = jnp.where(row == r, t, acc)
            o_x[b, z, h] = (acc + p_new * v_new).astype(BF16)
        for k in (2, 1, 3):
            o_copy(z, lax.rem(z + k, NZ), it).start()

    where = lax.broadcasted_iota(jnp.int32, (slots, hd), 0)

    def patch(h, b):
        for r in range(NP):
            hit = where == lens[b * NP + r]
            for i, ref in enumerate((k_out, v_out)):
                fresh = jnp.broadcast_to(new_kv[i, h, b, r:r + 1, :], (slots, hd))
                ref[b * NP + r, h] = jnp.where(hit, fresh, ref[b * NP + r, h].astype(F32)).astype(BF16)

    mine = pl.ds(pl.multiple_of(core * side, side), side)
    other = pl.ds(pl.multiple_of((1 - core) * side, side), side)

    def a_copy(key, j):
        return remote(red.at[key, j, other], r1.at[key, j], a_s.at[key, j], a_r.at[key, j], tp=sib)

    def b_copy(key, j):
        return remote(s_buf.at[key, j], r2.at[key, j], b_s.at[key, j], b_r.at[key, j], tp=across)

    def c_copy(key, j, who):
        view = (h_mid, h_fin)[key // 2].at[key % 2, j, pl.ds(pl.multiple_of(who * side, side), side)]
        return remote(view, view, c_s.at[key, j], c_r.at[key, j], tp=sib)

    def o_gather(b):
        def wait(p, carry):
            it = b * n_pair + p
            for k in (1, 3, 2):
                o_copy(lax.rem(z + k, NZ), lax.rem(z + k, NZ), it).wait_recv()
            return carry

        lax.fori_loop(0, n_pair, wait, 0)
        o_cat[...] = jnp.concatenate([jnp.concatenate([o_x[b, d, h].astype(F32) for h in range(heads)], axis=1) for d in range(NZ)], axis=0).astype(BF16)

    def o_product(b, j):
        red[b, j] = jnp.dot(o_cat[...], wo_b[:, j * rcol:(j + 1) * rcol], preferred_element_type=F32)
        a_copy(b, j).start()

    def m_rows(b):
        return pl.ds(b * half, half)

    def stage_b(key):
        for j in range(n_red):
            a_copy(key, j).wait_recv()
            s_buf[key, j] = red[key, j, mine] + r1[key, j]
            b_copy(key, j).start()

    def stage_c(key):
        b = key % 2
        for j in range(n_red):
            b_copy(key, j).wait_recv()
            total = (s_buf[key, j] + r2[key, j]).astype(BF16).astype(F32)
            if key < 2:
                base = hid_p[pl.ds(pl.multiple_of(b * half + core * side, side), side), pl.ds(j * rcol, rcol)]
                h_mid[b, j, mine] = (base.astype(F32) + total).astype(BF16)
            else:
                h_fin[b, j, mine] = (h_mid[b, j, mine].astype(F32) + total).astype(BF16)
            c_copy(key, j, core).start()

    def stage_d(key):
        for j in range(n_red):
            c_copy(key, j, 1 - core).wait_recv()
        if key < 2:
            x = jnp.concatenate([h_mid[key, j].astype(F32) for j in range(n_red)], axis=1)
            local_norm(x, g2[...].astype(F32).reshape(1, width), 1 + key, key * half)

    def a_slot(t, carry):
        @pl.when(t < n_pair)
        def _():
            for e in range(2):
                h = 2 * t + e
                for i in range(3):
                    load_w(i, h).wait()
                    y = jnp.dot(x_buf[...], wbuf[i, h], preferred_element_type=F32)
                    for b in range(2):
                        for d in range(NZ):
                            lo = (b * NZ + d) * NP
                            part[d, b * n_pair + t, :, (3 * e + i) * hd:(3 * e + i + 1) * hd] = y[lo:lo + NP]

        p = t - A_LAG * z

        @pl.when(p == 0)
        def _():
            relay_stat(0, 0, (0, 1))

        @pl.when((p >= 0) & (p < n_a))
        def _():
            b = p // n_pair
            for d in (3, 2, 1):
                @pl.when((z > 0) & (z <= d))
                def _(d=d):
                    right(d, p).wait_recv()

                @pl.when((z > 0) & (z < d))
                def _(d=d):
                    part[d, p] = part[d, p] * repeat(fac[0, b, d], 6) + rbuf[d, p] * repeat(fac[1, b, d], 6)

                @pl.when(z < d)
                def _(d=d):
                    right(d, p).start()

        q = t - A_LAG * (NZ - 1 - z)

        @pl.when(q == 0)
        def _():
            relay_stat(0, 1, (0, 1))

        @pl.when((q >= 0) & (q < n_a))
        def _():
            b = q // n_pair
            for d in (0, 1, 2):
                @pl.when((z < NZ - 1) & (z >= d))
                def _(d=d):
                    left(d, q).wait_recv()

                @pl.when((z < NZ - 1) & (z > d))
                def _(d=d):
                    part[d, q] = part[d, q] * repeat(fac[2, b, d], 6) + lbuf[d, q] * repeat(fac[3, b, d], 6)

                @pl.when(z > d)
                def _(d=d):
                    left(d, q).start()

        f = t - A_LAG * jnp.maximum(z, NZ - 1 - z)

        @pl.when(f == 0)
        def _():
            own = own_sq[0]
            scale = inv((cum_in[0, 0] + own) + cum_in[0, 1])
            put_fac(4, scale / inv(own), (0, 1))
            put_fac(5, scale / inv(cum_in[0, 0]), (0, 1))
            put_fac(6, scale / inv(cum_in[0, 1]), (0, 1))

        @pl.when((f >= 0) & (f < n_a))
        def _():
            attend(f)

        o_at = n_pair - 1 + A_LAG * (NZ - 1) + 2

        @pl.when(t == o_at)
        def _():
            load_o.wait()
            o_gather(0)
            for j in range(n_red):
                o_product(0, j)

        @pl.when(t == o_at + 1)
        def _():
            stage_b(0)

        return carry

    a_end = max(n_a + A_LAG * (NZ - 1), n_pair + A_LAG * (NZ - 1) + 3)
    lax.fori_loop(0, a_end, a_slot, 0)

    def patch_x(h, carry):
        patch(h, 0)
        return carry

    lax.fori_loop(0, heads, patch_x, 0)
    stage_c(0)
    stage_d(0)

    def right2(c):
        return remote(pbuf.at[c, 1], rbuf2.at[c], rs2.at[c], rr2.at[c], dm=nxt)

    def left2(c):
        return remote(pbuf.at[c, 0], lbuf2.at[c], ls2.at[c], lr2.at[c], dm=prv)

    def valid(c):
        return ((c >= 0) & (c < n_col)) | ((c >= second) & (c < n_e))

    def half_of(c):
        b = c // second
        return b, c - b * second

    def m_view(c, high):
        b, k = half_of(c)
        return mbuf.at[pl.ds(pl.multiple_of(b * half + high * side, side), side), pl.ds(pl.multiple_of(k * COL, COL), COL)]

    def m_left(c):
        return remote(m_view(c, 1), m_view(c, 1), mr_s.at[c], mr_r.at[c], dm=prv)

    def m_right(c):
        return remote(m_view(c, 0), m_view(c, 0), ml_s.at[c], ml_r.at[c], dm=nxt)

    def m_far(c, high, k):
        to = (NZ - 1 - k) if high else k
        recv = mr_r if high else ml_r
        return remote(m_view(c, high), m_view(c, high), far_s.at[high, c - direct_from, k - 2], recv.at[c], dm=to)

    def gated(a):
        g, u = a[:, :COL], a[:, COL:]
        return (g * (1.0 / (1.0 + jnp.exp(-g))) * u).astype(BF16)

    def wide(i, b, first):
        f = jnp.concatenate([fac[i, b, first], fac[i, b, first + 1]], axis=0)
        return repeat(f, 2 * COL // 128)

    def finish(c, high):
        b, k = half_of(c)
        mbuf[pl.ds(pl.multiple_of(b * half + high * side, side), side), pl.ds(pl.multiple_of(k * COL, COL), COL)] = gated(pbuf[c, high])

        @pl.when(c >= direct_from)
        def _():
            m_far(c, high, 3).start()
            m_far(c, high, 2).start()

        (m_left if high else m_right)(c).start()

    def e_slot(t, carry):
        @pl.when(valid(t))
        def _():
            b, k = half_of(t)

            @pl.when(b == 0)
            def _():
                load(0, k).wait()
                load(1, k).wait()

            cols = pl.ds(pl.multiple_of(k * COL, COL), COL)
            x = x_buf[pl.ds(pl.multiple_of(b * half, half), half), :]
            g = jnp.dot(x, wg_b[:, cols], preferred_element_type=F32)
            u = jnp.dot(x, wu_b[:, cols], preferred_element_type=F32)
            for s in range(2):
                pbuf[t, s, :, 0:COL] = g[s * side:(s + 1) * side]
                pbuf[t, s, :, COL:] = u[s * side:(s + 1) * side]

        c = t - E_LAG * z
        for step, first in ((1, 0), (2, second)):
            @pl.when(c == first)
            def _(step=step):
                relay_stat(step, 0, (step - 1,))

        @pl.when(valid(c))
        def _():
            b = c // second

            @pl.when(z > 0)
            def _():
                right2(c).wait_recv()
                pbuf[c, 1] = pbuf[c, 1] * wide(0, b, 2) + rbuf2[c] * wide(1, b, 2)

            @pl.when(z < NZ - 1)
            def _():
                right2(c).start()

            @pl.when(z == NZ - 1)
            def _():
                finish(c, 1)

        d = t - E_LAG * (NZ - 1 - z)
        for step, first in ((1, 0), (2, second)):
            @pl.when(d == first)
            def _(step=step):
                relay_stat(step, 1, (step - 1,))

        @pl.when(valid(d))
        def _():
            b = d // second

            @pl.when(z < NZ - 1)
            def _():
                left2(d).wait_recv()
                pbuf[d, 0] = pbuf[d, 0] * wide(2, b, 0) + lbuf2[d] * wide(3, b, 0)

            @pl.when(z > 0)
            def _():
                left2(d).start()

            @pl.when(z == 0)
            def _():
                finish(d, 0)

        e = t - E_LAG * (2 * NZ - 2 - z)

        @pl.when(valid(e) & (z < NZ - 1))
        def _():
            m_left(e).wait_recv()

            @pl.when((z > 0) & (e < direct_from))
            def _():
                m_left(e).start()

        f = t - E_LAG * (NZ - 1 + z)

        @pl.when(valid(f) & (z > 0))
        def _():
            m_right(f).wait_recv()

            @pl.when((z < NZ - 1) & (f < direct_from))
            def _():
                m_right(f).start()

        @pl.when(t == 1)
        def _():
            o_gather(1)
            for j in range(n_red):
                o_product(1, j)

        @pl.when(t == 2)
        def _():
            stage_b(1)

        @pl.when(t == 5)
        def _():
            stage_c(1)

        @pl.when(t == 7)
        def _():
            stage_d(1)

        @pl.when((t >= n_e) & (t < n_e + heads))
        def _():
            patch(t - n_e, 1)

        down = n_col + 2 * trip
        for j in range(n_red):
            @pl.when(t == down + j)
            def _(j=j):
                if j == 0:
                    load_d.wait()
                red[2, j] = jnp.dot(mbuf[m_rows(0), :], wd_b[:, j * rcol:(j + 1) * rcol], preferred_element_type=F32)
                a_copy(2, j).start()

        @pl.when(t == down + 2)
        def _():
            stage_b(2)

        @pl.when(t == down + 5)
        def _():
            stage_c(2)

        @pl.when(t == down + 7)
        def _():
            stage_d(2)

        late = second + early + 2 * trip
        for j in range(n_red):
            @pl.when(t == late + j)
            def _(j=j):
                red[3, j] = jnp.dot(mbuf[m_rows(1), 0:early * COL], wd_b[0:early * COL, j * rcol:(j + 1) * rcol], preferred_element_type=F32)

        return carry

    lax.fori_loop(0, max(n_e + 2 * trip, second + early + n_red + 2 * trip, n_e + heads, n_col + 2 * trip + 8), e_slot, 0)
    for j in range(n_red):
        red[3, j] = red[3, j] + jnp.dot(mbuf[m_rows(1), early * COL:], wd_b[early * COL:, j * rcol:(j + 1) * rcol], preferred_element_type=F32)
        a_copy(3, j).start()
    stage_b(3)

    def drain_a(p, carry):
        for d in range(NZ):
            @pl.when(z < d)
            def _(d=d):
                right(d, p).wait_send()

            @pl.when(z > d)
            def _(d=d):
                left(d, p).wait_send()

        for k in range(1, NZ):
            o_copy(z, lax.rem(z + k, NZ), p).wait_send()
        return carry

    lax.fori_loop(0, n_a, drain_a, 0)

    def drain_e(c, carry):
        @pl.when(valid(c))
        def _():
            @pl.when(z < NZ - 1)
            def _():
                right2(c).wait_send()

            @pl.when((z == 0) | ((z < NZ - 1) & (c < direct_from)))
            def _():
                m_right(c).wait_send()

            @pl.when(z > 0)
            def _():
                left2(c).wait_send()

            @pl.when((z == NZ - 1) | ((z > 0) & (c < direct_from)))
            def _():
                m_left(c).wait_send()

            for high in range(2):
                @pl.when((c >= direct_from) & (z == (NZ - 1) * high))
                def _(high=high):
                    m_far(c, high, 2).wait_send()
                    m_far(c, high, 3).wait_send()

        return carry

    lax.fori_loop(0, n_e, drain_e, 0)
    for step in range(3):
        @pl.when(z < NZ - 1)
        def _(step=step):
            stat(step, 0).wait_send()

        @pl.when(z > 0)
        def _(step=step):
            stat(step, 1).wait_send()

    stage_c(3)
    stage_d(3)
    for b in range(2):
        y = jnp.concatenate([h_fin[b, j].astype(F32) for j in range(n_red)], axis=1)
        if b == 0:
            ys = [y]
        else:
            ys.append(y)
    out[...] = jnp.concatenate([ys[b][d * NP:(d + 1) * NP] for d in range(NZ) for b in range(2)], axis=0).astype(BF16)
    for key in range(4):
        for j in range(n_red):
            a_copy(key, j).wait_send()
            b_copy(key, j).wait_send()
            c_copy(key, j, core).wait_send()


def layer_call(hid, g1, g2, wq, wk, wv, wo, wg, wu, wd, kc, vc, lens, cos, sin):
    rows, width = hid.shape
    heads, hd = wq.shape[0], wq.shape[2]
    slots = kc.shape[2]
    ff = wg.shape[1]
    half = rows // 2
    side = half // 2
    n_a = heads
    n_col = ff // COL
    n_e = max(n_col, 8) + n_col
    n_red = 2
    rcol = width // n_red
    hbm = pl.BlockSpec(memory_space=pl.ANY)
    vm = pl.BlockSpec(memory_space=pltpu.VMEM)
    dma = pltpu.SemaphoreType.DMA
    sums = pltpu.VMEM((NZ, n_a, NP, 6 * hd), F32)
    act = pltpu.VMEM((rows, width), BF16)
    half_red = pltpu.VMEM((4, n_red, side, rcol), F32)
    h_halves = pltpu.VMEM((2, n_red, half, rcol), BF16)
    return pl.pallas_call(
        layer_kernel,
        name='layer',
        out_shape=[pltpu.VMEM((rows, width), BF16), pltpu.VMEM(kc.shape, BF16), pltpu.VMEM(vc.shape, BF16)],
        in_specs=[hbm] * 15,
        out_specs=[vm, vm, vm],
        scratch_shapes=[
            act, pltpu.VMEM(g1.shape, g1.dtype), pltpu.VMEM(g2.shape, g2.dtype), pltpu.SMEM(lens.shape, jnp.int32), pltpu.VMEM(cos.shape, F32), pltpu.VMEM(sin.shape, F32),
            act, pltpu.VMEM((2, NP, slots), jnp.int32), pltpu.VMEM((2, 2, NP, hd), F32),
            pltpu.VMEM((3, heads, width, hd), BF16),
            pltpu.VMEM(wo.shape, BF16), pltpu.VMEM(wg.shape, BF16), pltpu.VMEM(wu.shape, BF16), pltpu.VMEM(wd.shape, BF16),
            sums, sums, sums,
            act, pltpu.VMEM((2, NZ, heads, NP, hd), BF16), pltpu.VMEM((half, width), BF16),
            pltpu.VMEM((2, heads, 2, NP, hd), F32),
            pltpu.VMEM((4, n_red, half, rcol), F32),
            half_red, half_red, half_red,
            h_halves, h_halves,
            pltpu.VMEM((n_e, 2, side, 2 * COL), F32),
            pltpu.VMEM((n_e, side, 2 * COL), F32),
            pltpu.VMEM((n_e, side, 2 * COL), F32),
            pltpu.VMEM((rows, ff), BF16),
            pltpu.VMEM((3, 2, 8, 128), F32), pltpu.VMEM((3, 2, 8, 128), F32), pltpu.VMEM((3, 8, 128), F32),
            pltpu.VMEM((7, 2, NZ, NP, 128), F32),
            dma((6,)), dma((3, heads)), dma((2, heads)), dma((2,)), dma((2, n_col)),
            dma((NZ, n_a)), dma((NZ, n_a)), dma((NZ, n_a)), dma((NZ, n_a)),
            dma((n_a, NZ)), dma((n_a, NZ)),
            dma((4, n_red)), dma((4, n_red)), dma((4, n_red)), dma((4, n_red)), dma((4, n_red)), dma((4, n_red)),
            dma((3, 2)), dma((3, 2)),
            dma((n_e,)), dma((n_e,)), dma((n_e,)), dma((n_e,)),
            dma((n_e,)), dma((n_e,)), dma((n_e,)), dma((n_e,)),
            dma((2, DIRECT, 2)),
        ],
        compiler_params=pltpu.CompilerParams(collective_id=0, has_side_effects=True, vmem_limit_bytes=VMEM_KIB * 1024),
    )(hid, g1, g2, wq, wk, wv, wo, wg, wu, wd, kc, vc, lens, cos, sin)


VMEM_KIB = 49 * 1024


def solution(mesh):
    row_spec = P('dp', 'dm')
    cache_spec = P(('dp', 'dm'), None, 'tp', None)
    batch_spec = P(('dp', 'dm'))
    rope_spec = P(('dp', 'dm'), None)
    in_specs = (row_spec, P('dm', 'tp', None), P('dm', 'tp', None), P('dm', 'tp', None), P('tp', None, 'dm'), P('dm', 'tp'), P('dm', 'tp'), P('tp', 'dm'), P('dm'), P('dm'), cache_spec, cache_spec, batch_spec, rope_spec, rope_spec)
    out_specs = (row_spec, cache_spec, cache_spec)

    def local_layer(hidden, w_q, w_k, w_v, w_o, w_gate, w_up, w_down, norm_attn, norm_mlp, k_cache, v_cache, seq_lens, rope_cos, rope_sin):
        by_head = [w.transpose(1, 0, 2) for w in (w_q, w_k, w_v)]
        caches = [c.transpose(0, 2, 1, 3) for c in (k_cache, v_cache)]
        h_out, k_out, v_out = layer_call(hidden, norm_attn, norm_mlp, *by_head, w_o.reshape(-1, w_o.shape[-1]), w_gate, w_up, w_down, *caches, seq_lens, rope_cos, rope_sin)
        return h_out, k_out.transpose(0, 2, 1, 3), v_out.transpose(0, 2, 1, 3)

    return jax.shard_map(local_layer, mesh=mesh, in_specs=in_specs, out_specs=out_specs, check_vma=False)
```

time: 111 us -> 102 us (0.919)
  Pallas kernels: 105 us -> 95.7 us
    pallas_call x1, Pallas kernels: 105 us -> 95.7 us  [layer_call(): pl.pallas_call(layer_kernel, name='layer', out_shape=[pltpu.VMEM((rows, w...]
where the time goes in v4:
time: 102 us
  Pallas kernels  95.7 us (94%)
  local copies, waits for them, and re-layouts  5.38 us (5%)
    pallas_call x1, Pallas kernels, layer_call(): pl.pallas_call(layer_kernel, name='layer', out_shape=[pltpu.VMEM((rows, w...  95.7 us
    unnamed x3, local copies, waits for them, and re-layouts  5.38 us

profile of v4, /device:TPU:0, one launch (start us, length us, event | category | flops | bytes accessed | tf_op | source)
XLA Modules:
  0.0 101.7 jit_solution(16450838807773294957)
XLA Ops:
  0.6 95.7 %layer.1 = (bf16[64,1280]{1,0:T(8,128)(2,1)S(1)}, bf16[16,10,128,128]{3,2,1,0:T(8,128)(2,1)S(1)}, bf16[16,10,128,128]{3,2,1,0:T(8,128)(2,1)S(1)}) custom-call(bf16[64,1280]{1,0:T(8,128)(2,1)} %hid_h.1, bf16[1280]{0:T(1024)(128)(2,1)} %g1_h.1, bf16[1280]{0:T(1024)(128)(2,1)} %g2_h.1, bf16[10,1280,128]{2,1,0:T(8,128)(2,1)} %bitcast.12, ...), custom_call_target="tpu_custom_call" | custom-call | tf_op jit(solution)/shard_map/layer/pallas_call | solution.py:686
  96.3 0.7 copy.21
  97.0 2.4 %copy.22 = bf16[16,128,10,128]{3,1,2,0:T(8,128)(2,1)} copy(bf16[16,128,10,128]{3,1,2,0:T(8,128)(2,1)S(1)} %bitcast.9) | data formatting | bytes 10485760
  99.3 2.4 %copy.23 = bf16[16,128,10,128]{3,1,2,0:T(8,128)(2,1)} copy(bf16[16,128,10,128]{3,1,2,0:T(8,128)(2,1)S(1)} %bitcast.8) | data formatting | bytes 10485760

commit v5 on v4

--- a/solution.py
+++ b/solution.py
@@ -63,7 +63,7 @@
     n_pair = heads // 2
     n_a = 2 * n_pair
     n_col = ff // COL
-    second = max(n_col, 8)
+    second = max(n_col, 9)
     n_e = second + n_col
     trip = E_LAG * (NZ - 1)
     n_grp = g_sem.shape[1]
@@ -132,15 +132,15 @@
     hid_p[...] = x0.astype(BF16)
     local_norm(x0, g1[...].astype(F32).reshape(1, width), 0, 0)
     cs, sn = cos[...], sin[...]
-    row = lax.broadcasted_iota(jnp.int32, (NP, slots), 0)
-    pos = lax.broadcasted_iota(jnp.int32, (NP, slots), 1)
+    row = lax.broadcasted_iota(jnp.int32, (2 * NP, slots), 0)
+    pos = lax.broadcasted_iota(jnp.int32, (2 * NP, slots), 1)
     for b in range(2):
-        part_cs, part_sn = cs[b * NP:(b + 1) * NP], sn[b * NP:(b + 1) * NP]
+        part_cs, part_sn = [jnp.concatenate([t[b * NP:(b + 1) * NP]] * 2, axis=0) for t in (cs, sn)]
         rope[0, b] = jnp.concatenate([part_cs, part_cs], axis=-1)
         rope[1, b] = jnp.concatenate([-part_sn, part_sn], axis=-1)
-        length = jnp.zeros((NP, slots), jnp.int32)
+        length = jnp.zeros((2 * NP, slots), jnp.int32)
         for r in range(NP):
-            length = jnp.where(row == r, lens[b * NP + r], length)
+            length = jnp.where((row == r) | (row == NP + r), lens[b * NP + r], length)
         len_v[b] = length
 
     def stat(step, way):
@@ -208,41 +208,44 @@
 
     def attend(it):
         b, p = split(it)
-        y6 = part[z, it] * repeat(fac[4, b, z], 6) + (rbuf[z, it] * repeat(fac[5, b, z], 6) + lbuf[z, it] * repeat(fac[6, b, z], 6))
+        y = part[z, it] * repeat(fac[4, b, z], 6) + (rbuf[z, it] * repeat(fac[5, b, z], 6) + lbuf[z, it] * repeat(fac[6, b, z], 6))
+
+        @pl.when(b == 0)
+        def _():
+            for e in range(2):
+                load_c(0, 2 * p + e).wait()
+                load_c(1, 2 * p + e).wait()
+
+        q, k, v_new = [jnp.concatenate([y[:, i * hd:(i + 1) * hd], y[:, (3 + i) * hd:(4 + i) * hd]], axis=0) for i in range(3)]
         cos2, sin2 = rope[0, b], rope[1, b]
         at_len = pos == len_v[b]
         seen = pos <= len_v[b]
+        q = (q * cos2 + pltpu.roll(q, hd // 2, 1) * sin2).astype(BF16)
+        k_new = (k * cos2 + pltpu.roll(k, hd // 2, 1) * sin2).astype(BF16).astype(F32)
+        v_new = v_new.astype(BF16).astype(F32)
+        s = jnp.zeros((2 * NP, slots), F32)
         for e in range(2):
-            h = 2 * p + e
-            y = y6[:, e * 3 * hd:(e + 1) * 3 * hd]
-            q, k = y[:, 0:hd], y[:, hd:2 * hd]
-            q = (q * cos2 + pltpu.roll(q, hd // 2, 1) * sin2).astype(BF16)
-            k_new = (k * cos2 + pltpu.roll(k, hd // 2, 1) * sin2).astype(BF16).astype(F32)
-            v_new = y[:, 2 * hd:].astype(BF16).astype(F32)
-            new_kv[0, h, b] = k_new
-            new_kv[1, h, b] = v_new
-
-            @pl.when(b == 0)
-            def _(h=h):
-                load_c(0, h).wait()
-                load_c(1, h).wait()
-
-            s = jnp.zeros((NP, slots), F32)
             for r in range(NP):
-                t = lax.dot_general(q, k_out[b * NP + r, h], (((1,), (1,)), ((), ())), preferred_element_type=F32)
-                s = jnp.where(row == r, t, s)
-            s_new = jnp.sum(q.astype(F32) * k_new, axis=-1, keepdims=True)
-            s = jnp.where(at_len, s_new, s) * (hd ** -0.5)
-            s = jnp.where(seen, s, -1e30)
-            ex = jnp.exp(s - jnp.max(s, axis=-1, keepdims=True))
-            prob = (ex / jnp.sum(ex, axis=-1, keepdims=True)).astype(BF16).astype(F32)
-            p_new = jnp.sum(jnp.where(at_len, prob, 0.0), axis=-1, keepdims=True)
-            p_old = jnp.where(at_len, 0.0, prob).astype(BF16)
-            acc = jnp.zeros((NP, hd), F32)
+                t = lax.dot_general(q, k_out[b * NP + r, 2 * p + e], (((1,), (1,)), ((), ())), preferred_element_type=F32)
+                s = jnp.where(row == e * NP + r, t, s)
+        s_new = jnp.sum(q.astype(F32) * k_new, axis=-1, keepdims=True)
+        s = jnp.where(at_len, s_new, s) * (hd ** -0.5)
+        s = jnp.where(seen, s, -1e30)
+        ex = jnp.exp(s - jnp.max(s, axis=-1, keepdims=True))
+        prob = (ex / jnp.sum(ex, axis=-1, keepdims=True)).astype(BF16).astype(F32)
+        p_new = jnp.sum(jnp.where(at_len, prob, 0.0), axis=-1, keepdims=True)
+        p_old = jnp.where(at_len, 0.0, prob).astype(BF16)
+        acc = jnp.zeros((2 * NP, hd), F32)
+        for e in range(2):
             for r in range(NP):
-                t = jnp.dot(p_old, v_out[b * NP + r, h], preferred_element_type=F32)
-                acc = jnp.where(row == r, t, acc)
-            o_x[b, z, h] = (acc + p_new * v_new).astype(BF16)
+                t = jnp.dot(p_old, v_out[b * NP + r, 2 * p + e], preferred_element_type=F32)
+                acc = jnp.where(row == e * NP + r, t, acc)
+        acc = acc + p_new * v_new
+        for e in range(2):
+            h, at = 2 * p + e, slice(e * NP, (e + 1) * NP)
+            new_kv[0, h, b] = k_new[at]
+            new_kv[1, h, b] = v_new[at]
+            o_x[b, z, h] = acc[at].astype(BF16)
         for k in (2, 1, 3):
             o_copy(z, lax.rem(z + k, NZ), it).start()
 
@@ -314,60 +317,64 @@
         @pl.when(t < n_pair)
         def _():
             for e in range(2):
+                for i in range(3):
+                    load_w(i, 2 * t + e).wait()
+            for e in range(2):
                 h = 2 * t + e
                 for i in range(3):
-                    load_w(i, h).wait()
                     y = jnp.dot(x_buf[...], wbuf[i, h], preferred_element_type=F32)
                     for b in range(2):
                         for d in range(NZ):
                             lo = (b * NZ + d) * NP
                             part[d, b * n_pair + t, :, (3 * e + i) * hd:(3 * e + i + 1) * hd] = y[lo:lo + NP]
 
-        p = t - A_LAG * z
-
-        @pl.when(p == 0)
+        @pl.when(t == A_LAG * z)
         def _():
             relay_stat(0, 0, (0, 1))
 
-        @pl.when((p >= 0) & (p < n_a))
-        def _():
-            b = p // n_pair
-            for d in (3, 2, 1):
+        for d in (3, 2, 1):
+            p = t - A_LAG * z - (NZ - 1 - d)
+
+            @pl.when((p >= 0) & (p < n_a))
+            def _(d=d, p=p):
+                b = p // n_pair
+
                 @pl.when((z > 0) & (z <= d))
-                def _(d=d):
+                def _():
                     right(d, p).wait_recv()
 
                 @pl.when((z > 0) & (z < d))
-                def _(d=d):
+                def _():
                     part[d, p] = part[d, p] * repeat(fac[0, b, d], 6) + rbuf[d, p] * repeat(fac[1, b, d], 6)
 
                 @pl.when(z < d)
-                def _(d=d):
+                def _():
                     right(d, p).start()
 
-        q = t - A_LAG * (NZ - 1 - z)
-
-        @pl.when(q == 0)
+        @pl.when(t == A_LAG * (NZ - 1 - z))
         def _():
             relay_stat(0, 1, (0, 1))
 
-        @pl.when((q >= 0) & (q < n_a))
-        def _():
-            b = q // n_pair
-            for d in (0, 1, 2):
+        for d in (0, 1, 2):
+            q = t - A_LAG * (NZ - 1 - z) - d
+
+            @pl.when((q >= 0) & (q < n_a))
+            def _(d=d, q=q):
+                b = q // n_pair
+
                 @pl.when((z < NZ - 1) & (z >= d))
-                def _(d=d):
+                def _():
                     left(d, q).wait_recv()
 
                 @pl.when((z < NZ - 1) & (z > d))
-                def _(d=d):
+                def _():
                     part[d, q] = part[d, q] * repeat(fac[2, b, d], 6) + lbuf[d, q] * repeat(fac[3, b, d], 6)
 
                 @pl.when(z > d)
-                def _(d=d):
+                def _():
                     left(d, q).start()
 
-        f = t - A_LAG * jnp.maximum(z, NZ - 1 - z)
+        f = t - jnp.maximum(A_LAG * z + NZ - 1 - z, A_LAG * (NZ - 1 - z) + z)
 
         @pl.when(f == 0)
         def _():
@@ -548,11 +555,11 @@
         def _():
             stage_b(1)
 
-        @pl.when(t == 5)
+        @pl.when(t == 6)
         def _():
             stage_c(1)
 
-        @pl.when(t == 7)
+        @pl.when(t == 8)
         def _():
             stage_d(1)
 
@@ -573,14 +580,6 @@
         def _():
             stage_b(2)
 
-        @pl.when(t == down + 5)
-        def _():
-            stage_c(2)
-
-        @pl.when(t == down + 7)
-        def _():
-            stage_d(2)
-
         late = second + early + 2 * trip
         for j in range(n_red):
             @pl.when(t == late + j)
@@ -589,11 +588,13 @@
 
         return carry
 
-    lax.fori_loop(0, max(n_e + 2 * trip, second + early + n_red + 2 * trip, n_e + heads, n_col + 2 * trip + 8), e_slot, 0)
+    lax.fori_loop(0, max(n_e + 2 * trip, second + early + n_red + 2 * trip, n_e + heads, n_col + 2 * trip + 3), e_slot, 0)
     for j in range(n_red):
         red[3, j] = red[3, j] + jnp.dot(mbuf[m_rows(1), early * COL:], wd_b[early * COL:, j * rcol:(j + 1) * rcol], preferred_element_type=F32)
         a_copy(3, j).start()
+    stage_c(2)
     stage_b(3)
+    stage_d(2)
 
     def drain_a(p, carry):
         for d in range(NZ):
@@ -673,7 +674,7 @@
     side = half // 2
     n_a = heads
     n_col = ff // COL
-    n_e = max(n_col, 8) + n_col
+    n_e = max(n_col, 9) + n_col
     n_red = 2
     rcol = width // n_red
     hbm = pl.BlockSpec(memory_space=pl.ANY)
@@ -691,7 +692,7 @@
         out_specs=[vm, vm, vm],
         scratch_shapes=[
             act, pltpu.VMEM(g1.shape, g1.dtype), pltpu.VMEM(g2.shape, g2.dtype), pltpu.SMEM(lens.shape, jnp.int32), pltpu.VMEM(cos.shape, F32), pltpu.VMEM(sin.shape, F32),
-            act, pltpu.VMEM((2, NP, slots), jnp.int32), pltpu.VMEM((2, 2, NP, hd), F32),
+            act, pltpu.VMEM((2, 2 * NP, slots), jnp.int32), pltpu.VMEM((2, 2, 2 * NP, hd), F32),
             pltpu.VMEM((3, heads, width, hd), BF16),
             pltpu.VMEM(wo.shape, BF16), pltpu.VMEM(wg.shape, BF16), pltpu.VMEM(wu.shape, BF16), pltpu.VMEM(wd.shape, BF16),
             sums, sums, sums,

time: 102 us -> 96.3 us (0.944)
  Pallas kernels: 95.7 us -> 90.2 us
    pallas_call x1, Pallas kernels: 95.7 us -> 90.2 us  [layer_call(): pl.pallas_call(layer_kernel, name='layer', out_shape=[pltpu.VMEM((rows, w...]
where the time goes in v5:
time: 96.3 us; the launch traced here: 96.2 us
  Pallas kernels  90.2 us (94%)
  local copies, waits for them, and re-layouts  5.38 us (6%)
    pallas_call x1, Pallas kernels, layer_call(): pl.pallas_call(layer_kernel, name='layer', out_shape=[pltpu.VMEM((rows, w...  90.2 us
    unnamed x3, local copies, waits for them, and re-layouts  5.38 us

profile of v5, /device:TPU:0, one launch (start us, length us, event | category | flops | bytes accessed | tf_op | source)
XLA Modules:
  0.0 96.2 jit_solution(12587899917891260685)
XLA Ops:
  0.6 90.2 %layer.1 = (bf16[64,1280]{1,0:T(8,128)(2,1)S(1)}, bf16[16,10,128,128]{3,2,1,0:T(8,128)(2,1)S(1)}, bf16[16,10,128,128]{3,2,1,0:T(8,128)(2,1)S(1)}) custom-call(bf16[64,1280]{1,0:T(8,128)(2,1)} %hid_h.1, bf16[1280]{0:T(1024)(128)(2,1)} %g1_h.1, bf16[1280]{0:T(1024)(128)(2,1)} %g2_h.1, bf16[10,1280,128]{2,1,0:T(8,128)(2,1)} %bitcast.12, ...), custom_call_target="tpu_custom_call" | custom-call | tf_op jit(solution)/shard_map/layer/pallas_call | solution.py:687
  90.8 0.7 copy.21
  91.5 2.4 %copy.22 = bf16[16,128,10,128]{3,1,2,0:T(8,128)(2,1)} copy(bf16[16,128,10,128]{3,1,2,0:T(8,128)(2,1)S(1)} %bitcast.9) | data formatting | bytes 10485760
  93.8 2.4 %copy.23 = bf16[16,128,10,128]{3,1,2,0:T(8,128)(2,1)} copy(bf16[16,128,10,128]{3,1,2,0:T(8,128)(2,1)S(1)} %bitcast.8) | data formatting | bytes 10485760

commit v6 on v5

--- a/solution.py
+++ b/solution.py
@@ -12,6 +12,8 @@
 NZ = 4
 NP = 8
 A_LAG = 2
+FAR = 2
+X_LAG = 5
 E_LAG = 3
 COL = 384
 DIRECT = 4
@@ -35,19 +37,19 @@
     return jnp.broadcast_to(packed, (8, 128))
 
 
-def unpack_rows(tile, rows):
+def unpack_rows(tile, rows, first=0):
     lane = lax.broadcasted_iota(jnp.int32, (rows, 128), 1)
     row = lax.broadcasted_iota(jnp.int32, (rows, 128), 0)
     wide = jnp.broadcast_to(tile[0:1], (rows, 128))
-    return jnp.sum(jnp.where(lane == row, wide, 0.0), axis=1, keepdims=True)
+    return jnp.sum(jnp.where(lane == row + first, wide, 0.0), axis=1, keepdims=True)
 
 
 def layer_kernel(hid_h, g1_h, g2_h, wq, wk, wv, wo, wg, wu, wd, kc, vc, lens_h, cos_h, sin_h,
                  out, k_out, v_out,
                  hid, g1, g2, lens, cos, sin, hid_p, len_v, rope, wbuf, wo_b, wg_b, wu_b, wd_b,
-                 part, rbuf, lbuf, x_buf, o_x, o_cat, new_kv, red, r1, s_buf, r2, h_mid, h_fin, pbuf, rbuf2, lbuf2, mbuf,
-                 cum_in, cum_out, own_sq, fac,
-                 s_sem, w_sem, c_sem, b_sem, g_sem, rs, rr, ls, lr, o_s, o_r, a_s, a_r, b_s, b_r, c_s, c_r,
+                 part, rbuf, lbuf, dbuf, x_buf, o_x, o_cat, new_kv, red, r1, s_buf, r2, h_mid, h_fin, pbuf, rbuf2, lbuf2, mbuf,
+                 cum_in, cum_out, own_sq, sq_all, fac,
+                 s_sem, w_sem, c_sem, b_sem, g_sem, rs, rr, ls, lr, dx_s, dx_r, sq_s, sq_r, o_s, o_r, a_s, a_r, b_s, b_r, c_s, c_r,
                  q_s, q_r, rs2, rr2, ls2, lr2, mr_s, mr_r, ml_s, ml_r, far_s):
     z = lax.axis_index('dm')
     tp = lax.axis_index('tp')
@@ -146,9 +148,9 @@
     def stat(step, way):
         return remote(cum_out.at[step, way], cum_in.at[step, way], q_s.at[step, way], q_r.at[step, way], dm=(nxt, prv)[way])
 
-    def put_fac(i, tile, halves):
+    def put_fac(i, tile, halves, first=0):
         n = len(halves) * half
-        wide = jnp.broadcast_to(unpack_rows(tile, n), (n, 128))
+        wide = jnp.broadcast_to(unpack_rows(tile, n, first), (n, 128))
         for k, b in enumerate(halves):
             for d in range(NZ):
                 lo = (k * NZ + d) * NP
@@ -186,7 +188,34 @@
     def _():
         lbuf[NZ - 1] = jnp.zeros(lbuf.shape[1:], F32)
 
+    def sq_copy(src, to):
+        return remote(sq_all.at[src], sq_all.at[src], sq_s.at[to], sq_r.at[src], dm=to)
+
+    sq_all[z] = own_sq[0]
     pl.semaphore_wait(sem, NZ + 1)
+    for k in (2, 1, 3):
+        sq_copy(z, lax.rem(z + k, NZ)).start()
+
+    def a_stats():
+        for k in (1, 3, 2):
+            sq_copy(lax.rem(z + k, NZ), lax.rem(z + k, NZ)).wait_recv()
+        none = jnp.zeros((8, 128), F32)
+        before, after, own = none, none, own_sq[0]
+        for j in range(NZ):
+            before = before + jnp.where(j < z, sq_all[j], 0.0)
+            after = after + jnp.where(j > z, sq_all[j], 0.0)
+        total = inv((before + own) + after)
+        for i, other_side in enumerate((before, after)):
+            scale = inv(other_side + own)
+            put_fac(2 * i, scale / inv(own), (1,), half)
+            put_fac(2 * i + 1, scale / inv(other_side), (1,), half)
+            put_fac(5 + i, total / inv(other_side), (1,), half)
+        put_fac(4, total / inv(own), (1,), half)
+        for j in range(NZ):
+            put_fac(7 + j, total / inv(sq_all[j]), (0,))
+
+    def x_copy(src, to, p):
+        return remote(part.at[to, p], dbuf.at[src, p], dx_s.at[p, to], dx_r.at[p, src], dm=to)
 
     def right(d, p):
         return remote(part.at[d, p], rbuf.at[d, p], rs.at[d, p], rr.at[d, p], dm=nxt)
@@ -206,16 +235,21 @@
     def repeat(f, n):
         return jnp.concatenate([f] * n, axis=1)
 
-    def attend(it):
+    def attend_x(it):
+        for k in (1, 3, 2):
+            x_copy(lax.rem(z + k, NZ), lax.rem(z + k, NZ), it).wait_recv()
+        for e in range(2):
+            load_c(0, 2 * it + e).wait()
+            load_c(1, 2 * it + e).wait()
+        dbuf[z, it] = part[z, it]
+        terms = [dbuf[j, it] * repeat(fac[7 + j, 0, z], 6) for j in range(NZ)]
+        attend(it, (terms[0] + terms[1]) + (terms[2] + terms[3]))
+
+    def attend_y(it):
+        attend(it, part[z, it] * repeat(fac[4, 1, z], 6) + (rbuf[z, it] * repeat(fac[5, 1, z], 6) + lbuf[z, it] * repeat(fac[6, 1, z], 6)))
+
+    def attend(it, y):
         b, p = split(it)
-        y = part[z, it] * repeat(fac[4, b, z], 6) + (rbuf[z, it] * repeat(fac[5, b, z], 6) + lbuf[z, it] * repeat(fac[6, b, z], 6))
-
-        @pl.when(b == 0)
-        def _():
-            for e in range(2):
-                load_c(0, 2 * p + e).wait()
-                load_c(1, 2 * p + e).wait()
-
         q, k, v_new = [jnp.concatenate([y[:, i * hd:(i + 1) * hd], y[:, (3 + i) * hd:(4 + i) * hd]], axis=0) for i in range(3)]
         cos2, sin2 = rope[0, b], rope[1, b]
         at_len = pos == len_v[b]
@@ -328,14 +362,19 @@
                             lo = (b * NZ + d) * NP
                             part[d, b * n_pair + t, :, (3 * e + i) * hd:(3 * e + i + 1) * hd] = y[lo:lo + NP]
 
-        @pl.when(t == A_LAG * z)
-        def _():
-            relay_stat(0, 0, (0, 1))
+            for d in (3, 0, 2, 1):
+                @pl.when(z != d)
+                def _(d=d):
+                    x_copy(z, d, t).start()
+
+        @pl.when(t == n_pair)
+        def _():
+            a_stats()
 
         for d in (3, 2, 1):
-            p = t - A_LAG * z - (NZ - 1 - d)
-
-            @pl.when((p >= 0) & (p < n_a))
+            p = t - A_LAG * z - FAR * (NZ - 1 - d)
+
+            @pl.when((p >= n_pair) & (p < n_a))
             def _(d=d, p=p):
                 b = p // n_pair
 
@@ -351,14 +390,10 @@
                 def _():
                     right(d, p).start()
 
-        @pl.when(t == A_LAG * (NZ - 1 - z))
-        def _():
-            relay_stat(0, 1, (0, 1))
-
         for d in (0, 1, 2):
-            q = t - A_LAG * (NZ - 1 - z) - d
-
-            @pl.when((q >= 0) & (q < n_a))
+            q = t - A_LAG * (NZ - 1 - z) - FAR * d
+
+            @pl.when((q >= n_pair) & (q < n_a))
             def _(d=d, q=q):
                 b = q // n_pair
 
@@ -374,21 +409,19 @@
                 def _():
                     left(d, q).start()
 
-        f = t - jnp.maximum(A_LAG * z + NZ - 1 - z, A_LAG * (NZ - 1 - z) + z)
-
-        @pl.when(f == 0)
-        def _():
-            own = own_sq[0]
-            scale = inv((cum_in[0, 0] + own) + cum_in[0, 1])
-            put_fac(4, scale / inv(own), (0, 1))
-            put_fac(5, scale / inv(cum_in[0, 0]), (0, 1))
-            put_fac(6, scale / inv(cum_in[0, 1]), (0, 1))
-
-        @pl.when((f >= 0) & (f < n_a))
-        def _():
-            attend(f)
-
-        o_at = n_pair - 1 + A_LAG * (NZ - 1) + 2
+        g = t - X_LAG
+
+        @pl.when((g >= 0) & (g < n_pair))
+        def _():
+            attend_x(g)
+
+        f = t - jnp.maximum(A_LAG * z + FAR * (NZ - 1 - z), A_LAG * (NZ - 1 - z) + FAR * z)
+
+        @pl.when((f >= n_pair) & (f < n_a))
+        def _():
+            attend_y(f)
+
+        o_at = n_pair - 1 + X_LAG + 2
 
         @pl.when(t == o_at)
         def _():
@@ -397,13 +430,13 @@
             for j in range(n_red):
                 o_product(0, j)
 
-        @pl.when(t == o_at + 1)
+        @pl.when(t == o_at + 2)
         def _():
             stage_b(0)
 
         return carry
 
-    a_end = max(n_a + A_LAG * (NZ - 1), n_pair + A_LAG * (NZ - 1) + 3)
+    a_end = max(n_a + max(A_LAG, FAR) * (NZ - 1), n_pair + X_LAG + 4)
     lax.fori_loop(0, a_end, a_slot, 0)
 
     def patch_x(h, carry):
@@ -598,13 +631,17 @@
 
     def drain_a(p, carry):
         for d in range(NZ):
-            @pl.when(z < d)
+            @pl.when((p >= n_pair) & (z < d))
             def _(d=d):
                 right(d, p).wait_send()
 
-            @pl.when(z > d)
+            @pl.when((p >= n_pair) & (z > d))
             def _(d=d):
                 left(d, p).wait_send()
+
+            @pl.when((p < n_pair) & (z != d))
+            def _(d=d):
+                x_copy(z, d, p).wait_send()
 
         for k in range(1, NZ):
             o_copy(z, lax.rem(z + k, NZ), p).wait_send()
@@ -640,7 +677,9 @@
         return carry
 
     lax.fori_loop(0, n_e, drain_e, 0)
-    for step in range(3):
+    for k in range(1, NZ):
+        sq_copy(z, lax.rem(z + k, NZ)).wait_send()
+    for step in (1, 2):
         @pl.when(z < NZ - 1)
         def _(step=step):
             stat(step, 0).wait_send()
@@ -695,7 +734,7 @@
             act, pltpu.VMEM((2, 2 * NP, slots), jnp.int32), pltpu.VMEM((2, 2, 2 * NP, hd), F32),
             pltpu.VMEM((3, heads, width, hd), BF16),
             pltpu.VMEM(wo.shape, BF16), pltpu.VMEM(wg.shape, BF16), pltpu.VMEM(wu.shape, BF16), pltpu.VMEM(wd.shape, BF16),
-            sums, sums, sums,
+            sums, sums, sums, pltpu.VMEM((NZ, heads // 2, NP, 6 * hd), F32),
             act, pltpu.VMEM((2, NZ, heads, NP, hd), BF16), pltpu.VMEM((half, width), BF16),
             pltpu.VMEM((2, heads, 2, NP, hd), F32),
             pltpu.VMEM((4, n_red, half, rcol), F32),
@@ -705,10 +744,11 @@
             pltpu.VMEM((n_e, side, 2 * COL), F32),
             pltpu.VMEM((n_e, side, 2 * COL), F32),
             pltpu.VMEM((rows, ff), BF16),
-            pltpu.VMEM((3, 2, 8, 128), F32), pltpu.VMEM((3, 2, 8, 128), F32), pltpu.VMEM((3, 8, 128), F32),
-            pltpu.VMEM((7, 2, NZ, NP, 128), F32),
+            pltpu.VMEM((3, 2, 8, 128), F32), pltpu.VMEM((3, 2, 8, 128), F32), pltpu.VMEM((3, 8, 128), F32), pltpu.VMEM((NZ, 8, 128), F32),
+            pltpu.VMEM((7 + NZ, 2, NZ, NP, 128), F32),
             dma((6,)), dma((3, heads)), dma((2, heads)), dma((2,)), dma((2, n_col)),
             dma((NZ, n_a)), dma((NZ, n_a)), dma((NZ, n_a)), dma((NZ, n_a)),
+            dma((heads // 2, NZ)), dma((heads // 2, NZ)), dma((NZ,)), dma((NZ,)),
             dma((n_a, NZ)), dma((n_a, NZ)),
             dma((4, n_red)), dma((4, n_red)), dma((4, n_red)), dma((4, n_red)), dma((4, n_red)), dma((4, n_red)),
             dma((3, 2)), dma((3, 2)),
@@ -723,6 +763,36 @@
 VMEM_KIB = 49 * 1024
 
 
+def flush_kernel(h_in, k_in, v_in, h_out, k_out, v_out, sem):
+    rows = k_in.shape[0] // FLUSH
+    copies = [pltpu.make_async_copy(h_in, h_out, sem.at[2, 0])]
+    for i in range(FLUSH):
+        at = pl.ds(i * rows, rows)
+        copies.append(pltpu.make_async_copy(k_in.at[at], k_out.at[at], sem.at[0, i]))
+        copies.append(pltpu.make_async_copy(v_in.at[at], v_out.at[at], sem.at[1, i]))
+    for cp in copies:
+        cp.start()
+    for cp in copies:
+        cp.wait()
+
+
+def flush_call(h, k, v):
+    vm = pl.BlockSpec(memory_space=pltpu.VMEM)
+    hbm = pl.BlockSpec(memory_space=pl.ANY)
+    return pl.pallas_call(
+        flush_kernel,
+        name='flush',
+        out_shape=[pltpu.HBM(a.shape, a.dtype) for a in (h, k, v)],
+        in_specs=[vm] * 3,
+        out_specs=[hbm] * 3,
+        scratch_shapes=[pltpu.SemaphoreType.DMA((3, FLUSH))],
+        compiler_params=pltpu.CompilerParams(vmem_limit_bytes=2**20),
+    )(h, k, v)
+
+
+FLUSH = 4
+
+
 def solution(mesh):
     row_spec = P('dp', 'dm')
     cache_spec = P(('dp', 'dm'), None, 'tp', None)
@@ -735,6 +805,7 @@
         by_head = [w.transpose(1, 0, 2) for w in (w_q, w_k, w_v)]
         caches = [c.transpose(0, 2, 1, 3) for c in (k_cache, v_cache)]
         h_out, k_out, v_out = layer_call(hidden, norm_attn, norm_mlp, *by_head, w_o.reshape(-1, w_o.shape[-1]), w_gate, w_up, w_down, *caches, seq_lens, rope_cos, rope_sin)
+        h_out, k_out, v_out = flush_call(h_out, k_out, v_out)
         return h_out, k_out.transpose(0, 2, 1, 3), v_out.transpose(0, 2, 1, 3)
 
     return jax.shard_map(local_layer, mesh=mesh, in_specs=in_specs, out_specs=out_specs, check_vma=False)

time: 96.3 us -> 95.4 us (level)
  local copies, waits for them, and re-layouts: 5.38 us -> 0 us
  Pallas kernels: 90.2 us -> 94.6 us
    unnamed x3 -> x0, local copies, waits for them, and re-layouts: 5.38 us -> none
    pallas_call x0 -> x1, Pallas kernels: none -> 4.13 us  [flush_call(): pl.pallas_call(flush_kernel, name='flush', out_shape=[pltpu.HBM(a.shape,...]
where the time goes in v6:
time: 95.4 us; the launch traced here: 95.3 us
  Pallas kernels  94.6 us (99%)
    pallas_call x1, Pallas kernels, layer_call(): pl.pallas_call(layer_kernel, name='layer', out_shape=[pltpu.VMEM((rows, w...  90.5 us
    pallas_call x1, Pallas kernels, flush_call(): pl.pallas_call(flush_kernel, name='flush', out_shape=[pltpu.HBM(a.shape,...  4.13 us

profile of v6, /device:TPU:0, one launch (start us, length us, event | category | flops | bytes accessed | tf_op | source)
XLA Modules:
  0.0 95.3 jit_solution(18388998953368124435)
XLA Ops:
  0.6 90.5 %layer.1 = (bf16[64,1280]{1,0:T(8,128)(2,1)S(1)}, bf16[16,10,128,128]{3,2,1,0:T(8,128)(2,1)S(1)}, bf16[16,10,128,128]{3,2,1,0:T(8,128)(2,1)S(1)}) custom-call(bf16[64,1280]{1,0:T(8,128)(2,1)} %hid_h.1, bf16[1280]{0:T(1024)(128)(2,1)} %g1_h.1, bf16[1280]{0:T(1024)(128)(2,1)} %g2_h.1, bf16[10,1280,128]{2,1,0:T(8,128)(2,1)} %bitcast.10, ...), custom_call_target="tpu_custom_call" | custom-call | tf_op jit(solution)/shard_map/layer/pallas_call | solution.py:726
  91.1 4.1 %flush.1 = (bf16[64,1280]{1,0:T(8,128)(2,1)}, bf16[16,10,128,128]{3,2,1,0:T(8,128)(2,1)}, bf16[16,10,128,128]{3,2,1,0:T(8,128)(2,1)}) custom-call(bf16[64,1280]{1,0:T(8,128)(2,1)S(1)} %get-tuple-element.9.h_in, bf16[16,10,128,128]{3,2,1,0:T(8,128)(2,1)S(1)} %get-tuple-element.10.k_in, bf16[16,10,128,128]{3,2,1,0:T(8,128)(2,1)S(1)} %get-tuple-element.11.v_in), custom_call_target="tpu_custom_call" | custom-call | tf_op jit(solution)/shard_map/flush/pallas_call | solution.py:782

commit v7 on v5

--- a/solution.py
+++ b/solution.py
@@ -92,20 +92,13 @@
 
     for cp in small:
         cp.start()
-    for h in range(heads):
-        for i in range(3):
-            load_w(i, h).start()
-        if h >= 2:
-            load_c(0, h - 2).start()
-            load_c(1, h - 2).start()
-    for h in range(max(heads - 2, 0), heads):
-        load_c(0, h).start()
-        load_c(1, h).start()
-    load_o.start()
-    for g in range(n_grp):
-        load(0, g).start()
-        load(1, g).start()
-    load_d.start()
+    def load_pair(p):
+        for e in range(2):
+            for i in range(3):
+                load_w(i, 2 * p + e).start()
+
+    for p in range(min(n_pair, 2)):
+        load_pair(p)
 
     sem = pltpu.get_barrier_semaphore()
     for k in range(1, NZ):
@@ -313,7 +306,32 @@
             x = jnp.concatenate([h_mid[key, j].astype(F32) for j in range(n_red)], axis=1)
             local_norm(x, g2[...].astype(F32).reshape(1, width), 1 + key, key * half)
 
+    a_end = max(n_a + A_LAG * (NZ - 1), n_pair + A_LAG * (NZ - 1) + 3, n_col + 7)
+
     def a_slot(t, carry):
+        @pl.when(t + 2 < n_pair)
+        def _():
+            load_pair(t + 2)
+
+        @pl.when((t >= 3) & (t < 3 + n_pair))
+        def _():
+            for e in range(2):
+                load_c(0, 2 * (t - 3) + e).start()
+                load_c(1, 2 * (t - 3) + e).start()
+
+        @pl.when(t == 7)
+        def _():
+            load_o.start()
+
+        @pl.when((t >= 7) & (t < 7 + n_col))
+        def _():
+            load(0, t - 7).start()
+            load(1, t - 7).start()
+
+        @pl.when(t == a_end - 1)
+        def _():
+            load_d.start()
+
         @pl.when(t < n_pair)
         def _():
             for e in range(2):
@@ -403,7 +421,6 @@
 
         return carry
 
-    a_end = max(n_a + A_LAG * (NZ - 1), n_pair + A_LAG * (NZ - 1) + 3)
     lax.fori_loop(0, a_end, a_slot, 0)
 
     def patch_x(h, carry):
@@ -723,6 +740,36 @@
 VMEM_KIB = 49 * 1024
 
 
+def flush_kernel(h_in, k_in, v_in, h_out, k_out, v_out, sem):
+    rows = k_in.shape[0] // FLUSH
+    copies = [pltpu.make_async_copy(h_in, h_out, sem.at[2, 0])]
+    for i in range(FLUSH):
+        at = pl.ds(i * rows, rows)
+        copies.append(pltpu.make_async_copy(k_in.at[at], k_out.at[at], sem.at[0, i]))
+        copies.append(pltpu.make_async_copy(v_in.at[at], v_out.at[at], sem.at[1, i]))
+    for cp in copies:
+        cp.start()
+    for cp in copies:
+        cp.wait()
+
+
+def flush_call(h, k, v):
+    vm = pl.BlockSpec(memory_space=pltpu.VMEM)
+    hbm = pl.BlockSpec(memory_space=pl.ANY)
+    return pl.pallas_call(
+        flush_kernel,
+        name='flush',
+        out_shape=[pltpu.HBM(a.shape, a.dtype) for a in (h, k, v)],
+        in_specs=[vm] * 3,
+        out_specs=[hbm] * 3,
+        scratch_shapes=[pltpu.SemaphoreType.DMA((3, FLUSH))],
+        compiler_params=pltpu.CompilerParams(vmem_limit_bytes=2**20),
+    )(h, k, v)
+
+
+FLUSH = 4
+
+
 def solution(mesh):
     row_spec = P('dp', 'dm')
     cache_spec = P(('dp', 'dm'), None, 'tp', None)
@@ -735,6 +782,7 @@
         by_head = [w.transpose(1, 0, 2) for w in (w_q, w_k, w_v)]
         caches = [c.transpose(0, 2, 1, 3) for c in (k_cache, v_cache)]
         h_out, k_out, v_out = layer_call(hidden, norm_attn, norm_mlp, *by_head, w_o.reshape(-1, w_o.shape[-1]), w_gate, w_up, w_down, *caches, seq_lens, rope_cos, rope_sin)
+        h_out, k_out, v_out = flush_call(h_out, k_out, v_out)
         return h_out, k_out.transpose(0, 2, 1, 3), v_out.transpose(0, 2, 1, 3)
 
     return jax.shard_map(local_layer, mesh=mesh, in_specs=in_specs, out_specs=out_specs, check_vma=False)

time: 96.3 us -> 86.3 us (0.90)
  local copies, waits for them, and re-layouts: 5.38 us -> 0 us
  Pallas kernels: 90.2 us -> 85.5 us
    pallas_call x1, Pallas kernels: 90.2 us -> 81.3 us  [layer_call(): pl.pallas_call(layer_kernel, name='layer', out_shape=[pltpu.VMEM((rows, w...]
    unnamed x3 -> x0, local copies, waits for them, and re-layouts: 5.38 us -> none
    pallas_call x0 -> x1, Pallas kernels: none -> 4.13 us  [flush_call(): pl.pallas_call(flush_kernel, name='flush', out_shape=[pltpu.HBM(a.shape,...]
where the time goes in v7:
time: 86.3 us; the launch traced here: 86.1 us
  Pallas kernels  85.5 us (99%)
    pallas_call x1, Pallas kernels, layer_call(): pl.pallas_call(layer_kernel, name='layer', out_shape=[pltpu.VMEM((rows, w...  81.3 us
    pallas_call x1, Pallas kernels, flush_call(): pl.pallas_call(flush_kernel, name='flush', out_shape=[pltpu.HBM(a.shape,...  4.13 us

profile of v7, /device:TPU:0, one launch (start us, length us, event | category | flops | bytes accessed | tf_op | source)
XLA Modules:
  0.0 86.1 jit_solution(2199180085626370512)
XLA Ops:
  0.6 81.3 %layer.1 = (bf16[64,1280]{1,0:T(8,128)(2,1)S(1)}, bf16[16,10,128,128]{3,2,1,0:T(8,128)(2,1)S(1)}, bf16[16,10,128,128]{3,2,1,0:T(8,128)(2,1)S(1)}) custom-call(bf16[64,1280]{1,0:T(8,128)(2,1)} %hid_h.1, bf16[1280]{0:T(1024)(128)(2,1)} %g1_h.1, bf16[1280]{0:T(1024)(128)(2,1)} %g2_h.1, bf16[10,1280,128]{2,1,0:T(8,128)(2,1)} %bitcast.10, ...), custom_call_target="tpu_custom_call" | custom-call | tf_op jit(solution)/shard_map/layer/pallas_call | solution.py:704
  82.0 4.1 %flush.1 = (bf16[64,1280]{1,0:T(8,128)(2,1)}, bf16[16,10,128,128]{3,2,1,0:T(8,128)(2,1)}, bf16[16,10,128,128]{3,2,1,0:T(8,128)(2,1)}) custom-call(bf16[64,1280]{1,0:T(8,128)(2,1)S(1)} %get-tuple-element.9.h_in, bf16[16,10,128,128]{3,2,1,0:T(8,128)(2,1)S(1)} %get-tuple-element.10.k_in, bf16[16,10,128,128]{3,2,1,0:T(8,128)(2,1)S(1)} %get-tuple-element.11.v_in), custom_call_target="tpu_custom_call" | custom-call | tf_op jit(solution)/shard_map/flush/pallas_call | solution.py:759

commit v8 on v6

--- a/solution.py
+++ b/solution.py
@@ -94,20 +94,13 @@
 
     for cp in small:
         cp.start()
-    for h in range(heads):
-        for i in range(3):
-            load_w(i, h).start()
-        if h >= 2:
-            load_c(0, h - 2).start()
-            load_c(1, h - 2).start()
-    for h in range(max(heads - 2, 0), heads):
-        load_c(0, h).start()
-        load_c(1, h).start()
-    load_o.start()
-    for g in range(n_grp):
-        load(0, g).start()
-        load(1, g).start()
-    load_d.start()
+    def load_pair(p):
+        for e in range(2):
+            for i in range(3):
+                load_w(i, 2 * p + e).start()
+
+    for p in range(min(n_pair, 2)):
+        load_pair(p)
 
     sem = pltpu.get_barrier_semaphore()
     for k in range(1, NZ):
@@ -347,7 +340,32 @@
             x = jnp.concatenate([h_mid[key, j].astype(F32) for j in range(n_red)], axis=1)
             local_norm(x, g2[...].astype(F32).reshape(1, width), 1 + key, key * half)
 
+    a_end = max(n_a + max(A_LAG, FAR) * (NZ - 1), n_pair + X_LAG + 4, n_col + 7)
+
     def a_slot(t, carry):
+        @pl.when(t + 2 < n_pair)
+        def _():
+            load_pair(t + 2)
+
+        @pl.when((t >= 3) & (t < 3 + n_pair))
+        def _():
+            for e in range(2):
+                load_c(0, 2 * (t - 3) + e).start()
+                load_c(1, 2 * (t - 3) + e).start()
+
+        @pl.when(t == 7)
+        def _():
+            load_o.start()
+
+        @pl.when((t >= 7) & (t < 7 + n_col))
+        def _():
+            load(0, t - 7).start()
+            load(1, t - 7).start()
+
+        @pl.when(t == a_end - 1)
+        def _():
+            load_d.start()
+
         @pl.when(t < n_pair)
         def _():
             for e in range(2):
@@ -436,7 +454,6 @@
 
         return carry
 
-    a_end = max(n_a + max(A_LAG, FAR) * (NZ - 1), n_pair + X_LAG + 4)
     lax.fori_loop(0, a_end, a_slot, 0)
 
     def patch_x(h, carry):

time: 95.4 us -> 86.7 us (0.909)
  Pallas kernels: 94.6 us -> 85.9 us
    pallas_call x1, Pallas kernels: 90.5 us -> 81.8 us  [layer_call(): pl.pallas_call(layer_kernel, name='layer', out_shape=[pltpu.VMEM((rows, w...]
where the time goes in v8:
time: 86.7 us; the launch traced here: 86.6 us
  Pallas kernels  85.9 us (99%)
    pallas_call x1, Pallas kernels, layer_call(): pl.pallas_call(layer_kernel, name='layer', out_shape=[pltpu.VMEM((rows, w...  81.8 us
    pallas_call x1, Pallas kernels, flush_call(): pl.pallas_call(flush_kernel, name='flush', out_shape=[pltpu.HBM(a.shape,...  4.13 us

profile of v8, /device:TPU:0, one launch (start us, length us, event | category | flops | bytes accessed | tf_op | source)
XLA Modules:
  0.0 86.6 jit_solution(15215660880024987216)
XLA Ops:
  0.6 81.8 %layer.1 = (bf16[64,1280]{1,0:T(8,128)(2,1)S(1)}, bf16[16,10,128,128]{3,2,1,0:T(8,128)(2,1)S(1)}, bf16[16,10,128,128]{3,2,1,0:T(8,128)(2,1)S(1)}) custom-call(bf16[64,1280]{1,0:T(8,128)(2,1)} %hid_h.1, bf16[1280]{0:T(1024)(128)(2,1)} %g1_h.1, bf16[1280]{0:T(1024)(128)(2,1)} %g2_h.1, bf16[10,1280,128]{2,1,0:T(8,128)(2,1)} %bitcast.10, ...), custom_call_target="tpu_custom_call" | custom-call | tf_op jit(solution)/shard_map/layer/pallas_call | solution.py:743
  82.5 4.1 %flush.1 = (bf16[64,1280]{1,0:T(8,128)(2,1)}, bf16[16,10,128,128]{3,2,1,0:T(8,128)(2,1)}, bf16[16,10,128,128]{3,2,1,0:T(8,128)(2,1)}) custom-call(bf16[64,1280]{1,0:T(8,128)(2,1)S(1)} %get-tuple-element.9.h_in, bf16[16,10,128,128]{3,2,1,0:T(8,128)(2,1)S(1)} %get-tuple-element.10.k_in, bf16[16,10,128,128]{3,2,1,0:T(8,128)(2,1)S(1)} %get-tuple-element.11.v_in), custom_call_target="tpu_custom_call" | custom-call | tf_op jit(solution)/shard_map/flush/pallas_call | solution.py:799
